TPU v7x, 32 devices: a whole 2x2x4 slice. The times are simulated.
32 devices in a mesh: gx: 16 (over z, y, core), gy: 2 (over x).
Axes of the slice: x: 2, y: 2, z: 4, core: 2. Of those that a mesh axis runs over, the one named last changes fastest.
Arguments:
- grid_field: bfloat16 [2, 256, 64, 512], P(None, 'gx', 'gy'), may hold values from -6 to 6
- spectral_weight: bfloat16 [128, 2, 512, 512], P('gx', None, None, 'gy'), may hold values from -0.1875 to 0.1875
- skip_weight: bfloat16 [512, 512], replicated, may hold values from -0.25 to 0.25
- inner_weight: bfloat16 [1024, 512], replicated, may hold values from -0.25 to 0.25
- outer_weight: bfloat16 [1024, 512], replicated, may hold values from -0.1875 to 0.1875
Outputs:
- layer_out: bfloat16 [2, 256, 64, 512], P(None, 'gx', 'gy')
All inputs are finite; a program needn't handle non-finite values.
Results may differ from a plain program's by a relative error of at most 0.0093.
Values may be sent and summed in bfloat16 or wider, within the bound.
No kernel may reach another device: no remote copies, remote signals or barrier semaphores. Data moves between devices by JAX's collectives and lax.ppermute only.
A program may use at most 64 MiB of HBM per device.

v0:
```python
import math

import jax
import jax.numpy as jnp
from jax import lax
from jax.sharding import PartitionSpec as P

KX = 16
KY = 8


def phase_table(row_ids, col_ids, total_rows, total_cols):
    x_modes = jnp.arange(KX, dtype=jnp.int32)
    y_modes = jnp.arange(KY, dtype=jnp.int32)
    x_phase = (x_modes[:, None] * row_ids[None, :] % total_rows).astype(jnp.float32) / total_rows
    y_phase = (y_modes[:, None] * col_ids[None, :] % total_cols).astype(jnp.float32) / total_cols
    angles = (x_phase[:, None, :, None] + y_phase[None, :, None, :]) * (2.0 * math.pi)
    angles = angles.reshape(KX * KY, row_ids.shape[0] * col_ids.shape[0])
    return jnp.concatenate([jnp.cos(angles), -jnp.sin(angles)], axis=0).astype(jnp.bfloat16)


def local(grid_field, spectral_weight, skip_weight, inner_weight, outer_weight):
    micro_count, row_count, col_count, width_count = grid_field.shape
    x_devices = lax.axis_size("gx")
    y_devices = lax.axis_size("gy")
    total_rows = row_count * x_devices
    total_cols = col_count * y_devices
    mode_count = KX * KY
    row_ids = lax.axis_index("gx") * row_count + jnp.arange(row_count, dtype=jnp.int32)
    col_ids = lax.axis_index("gy") * col_count + jnp.arange(col_count, dtype=jnp.int32)
    basis = phase_table(row_ids, col_ids, total_rows, total_cols)
    flat_rows = grid_field.reshape(micro_count, row_count * col_count, width_count)
    partial_value = jnp.einsum("kn,bnc->kbc", basis, flat_rows, preferred_element_type=jnp.float32)
    partial_value = partial_value.reshape(2, mode_count, micro_count, width_count)
    owned_modes = lax.psum_scatter(partial_value, "gx", scatter_dimension=1, tiled=True)
    owned_modes = lax.psum(owned_modes, "gy")
    spectrum = (owned_modes * (1.0 / math.sqrt(total_rows * total_cols))).astype(jnp.bfloat16)
    weight_re = spectral_weight[:, 0]
    weight_im = spectral_weight[:, 1]
    mixed_re = jnp.einsum(
        "mbc,mcd->mbd", spectrum[0], weight_re, preferred_element_type=jnp.float32
    ) - jnp.einsum("mbc,mcd->mbd", spectrum[1], weight_im, preferred_element_type=jnp.float32)
    mixed_im = jnp.einsum(
        "mbc,mcd->mbd", spectrum[0], weight_im, preferred_element_type=jnp.float32
    ) + jnp.einsum("mbc,mcd->mbd", spectrum[1], weight_re, preferred_element_type=jnp.float32)
    mixed_modes = jnp.stack([mixed_re, mixed_im]).astype(jnp.bfloat16)
    gathered = lax.all_gather(mixed_modes, "gy", axis=3, tiled=True)
    gathered = lax.all_gather(gathered, "gx", axis=1, tiled=True)
    gathered = gathered.reshape(2 * mode_count, micro_count, width_count)
    spectral = jnp.einsum("kn,kbc->bnc", basis, gathered, preferred_element_type=jnp.float32)
    spectral = spectral * (1.0 / math.sqrt(mode_count))
    skip_term = jnp.einsum(
        "bnc,cd->bnd", flat_rows, skip_weight, preferred_element_type=jnp.float32
    )
    active = jax.nn.gelu(spectral + skip_term).astype(jnp.bfloat16)
    hidden = jax.nn.gelu(
        jnp.einsum("bnc,hc->bnh", active, inner_weight, preferred_element_type=jnp.float32)
    )
    hidden = hidden.astype(jnp.bfloat16)
    feed_forward = jnp.einsum(
        "bnh,hc->bnc", hidden, outer_weight, preferred_element_type=jnp.float32
    )
    layer_out = (active.astype(jnp.float32) + feed_forward).astype(jnp.bfloat16)
    return layer_out.reshape(micro_count, row_count, col_count, width_count)


def solution(mesh):
    in_specs = (P(None, "gx", "gy", None), P("gx", None, None, "gy"), P(), P(), P())
    out_specs = P(None, "gx", "gy", None)
    return jax.shard_map(local, mesh=mesh, in_specs=in_specs, out_specs=out_specs, check_vma=False)
```

profile of v0, /device:TPU:0, one launch (start us, length us, event | category | flops | bytes accessed | tf_op | source)
XLA Modules:
  0.0 143.6 jit_solution(16070263595739132689)
XLA Ops:
  6.5 0.0 copy-start
  6.5 0.0 reduce-scatter.2.cloned.1.call-start
  6.6 4.1 %cosine_convert_fusion = (bf16[16,8,16,32]{3,2,1,0:T(8,128)(2,1)S(1)}, bf16[16,8,16,32]{3,2,1,0:T(8,128)(2,1)S(1)}) fusion(f32[8,32]{1,0:T(8,128)S(1)} %fusion.65, f32[16,16]{1,0:T(8,128)S(1)} %fusion.59), kind=kLoop, calls=%fused_computation.41 | loop fusion | flops 327680 | bytes 264192 | tf_op jit(solution)/shard_map/convert.7
  10.7 0.4 cos.7
  11.2 0.1 copy.14
  11.3 0.5 neg.7
  11.8 0.1 copy.15
  11.9 0.1 copy.16
  12.1 0.0 copy-done
  12.1 1.4 fusion.73
  13.5 0.0 reduce-scatter.2.cloned.1.call-update
  13.5 0.0 all-reduce.2.cloned.1.call-start
  13.6 60.4 %reduce-scatter.2.cloned.1.call-done = f32[2,8,2,512]{3,1,2,0:T(8,128)} async-done(((f32[2,128,2,512]{3,1,2,0:T(8,128)}), f32[2,8,2,512]{3,1,2,0:T(8,128)}) %reduce-scatter.2.cloned.1.call-update) | async-done | bytes 65552 | tf_op jit(solution)/shard_map/reduce_scatter | solution.py:35
  74.0 0.0 all-reduce.2.cloned.1.call-update
  74.0 1.7 %fusion.49 = f32[2,512,512]{2,1,0:T(8,128)S(1)} fusion(bf16[2,512,512]{2,1,0:T(8,128)(2,1)S(1)} %bitcast.69, bf16[512,512]{1,0:T(8,128)(2,1)} %param.7), kind=kOutput, calls=%fused_computation.43 | convolution fusion | flops 536870912 | bytes 3670016 | tf_op jit(solution)/shard_map/bnc,cd->bnd/dot_general | solution.py:52
  75.7 20.5 %all-reduce.2.cloned.1.call-done = f32[2,8,2,512]{3,1,2,0:T(8,128)} async-done(((f32[2,8,2,512]{3,1,2,0:T(8,128)}), f32[2,8,2,512]{3,1,2,0:T(8,128)}) %all-reduce.2.cloned.1.call-update) | async-done | bytes 65552 | tf_op jit(solution)/shard_map/psum | solution.py:36
  96.2 0.8 multiply_convert_fusion
  97.1 0.0 copy-start.1
  97.1 2.1 %fusion.18 = f32[8,2,256]{2,1,0:T(2,128)S(1)} fusion(bf16[8,2,512,256]{3,2,1,0:T(8,128)(2,1)} %param.6, bf16[8,2,512]{2,0,1:T(8,128)(2,1)S(1)} %get-tuple-element.5), kind=kOutput, calls=%fused_computation.20 | convolution fusion | flops 4194304 | bytes 2129920 | tf_op jit(solution)/shard_map/mbc,mcd->mbd/dot_general | solution.py:42
  99.2 2.0 %fusion.16 = f32[8,2,256]{2,1,0:T(2,128)S(1)} fusion(bf16[8,2,512,256]{3,2,1,0:T(8,128)(2,1)} %param.6, bf16[8,2,512]{2,0,1:T(8,128)(2,1)S(1)} %get-tuple-element.6), kind=kOutput, calls=%fused_computation.18 | convolution fusion | flops 4194304 | bytes 2129920 | tf_op jit(solution)/shard_map/mbc,mcd->mbd/dot_general | solution.py:43
  101.2 0.0 copy-done.1
  101.2 0.4 fusion.40
  101.6 0.4 fusion.43
  102.0 4.4 %all_gather.6 = bf16[2,8,2,512]{3,2,1,0:T(2,128)(2,1)S(1)} all-gather(bf16[2,8,2,256]{3,2,1,0:T(2,128)(2,1)S(1)} %pad_maximum_fusion.1), channel_id=1, replica_groups=mesh['gx'=16,'gy'=2] {'gy'}, dimensions={3}, use_global_device_ids=true | all-gather | bytes 49152 | tf_op jit(solution)/shard_map/all_gather | solution.py:47
  106.4 22.9 %all_gather.7 = bf16[2,128,2,512]{3,2,1,0:T(2,128)(2,1)S(1)} all-gather(bf16[2,8,2,512]{3,2,1,0:T(2,128)(2,1)S(1)} %all_gather.6), channel_id=1, replica_groups=mesh['gx'=16,'gy'=2] {'gx'}, dimensions={1}, use_global_device_ids=true | all-gather | bytes 557056 | tf_op jit(solution)/shard_map/all_gather | solution.py:48
  129.3 1.9 %fusion.15 = bf16[2,512,512]{2,1,0:T(8,128)(2,1)} fusion(f32[2,512,512]{2,1,0:T(8,128)S(1)} %fusion.49, bf16[256,2,512]{2,1,0:T(2,128)(2,1)S(1)} %bitcast.72, bf16[128,512]{0,1:T(8,128)(2,1)S(1)} %copy.15, bf16[128,512]{0,1:T(8,128)(2,1)S(1)} %copy.14), kind=kOutput, calls=%fused_computation.17 | convolution fusion | flops 274726912 | bytes 3932160 | tf_op jit(solution)/shard_map/kn,kbc->bnc/dot_general | solution.py:50
  131.2 5.5 %add_convert_fusion = bf16[2,512,512]{2,1,0:T(8,128)(2,1)} fusion(bf16[2,512,512]{2,1,0:T(8,128)(2,1)} %fusion.15, bf16[1024,512]{1,0:T(8,128)(2,1)} %param.9, bf16[1024,512]{1,0:T(8,128)(2,1)} %param.8), kind=kOutput, calls=%fused_computation.27 | convolution fusion | flops 2158493696 | bytes 4194304 | tf_op jit(solution)/shard_map/bnh,hc->bnc/dot_general | solution.py:60
  (7 shorter events, 0.1 us)
Async XLA Ops:
  6.5 5.5 %copy-start = (bf16[2,16,32,512]{3,2,1,0:T(8,128)(2,1)S(1)}, bf16[2,16,32,512]{3,2,1,0:T(8,128)(2,1)}, u32[]{:S(2)}) copy-start(bf16[2,16,32,512]{3,2,1,0:T(8,128)(2,1)} %param.5) | copy-start | bytes 3145732
  6.5 67.4 %reduce-scatter.2.cloned.1.call-start = ((), (), s32[]{:S(2)}) async-start(), calls=%async_computation.1 | async-start | bytes 1114112 | tf_op jit(solution)/shard_map/reduce_scatter | solution.py:35
  13.5 82.7 %all-reduce.2.cloned.1.call-start = ((), (), s32[]{:S(2)}) async-start(), calls=%async_computation.2 | async-start | bytes 131072 | tf_op jit(solution)/shard_map/psum | solution.py:36
  97.1 4.1 %copy-start.1 = (bf16[8,2,512,256]{3,2,1,0:T(8,128)(2,1)S(1)}, bf16[8,2,512,256]{3,2,1,0:T(8,128)(2,1)}, u32[]{:S(2)}) copy-start(bf16[8,2,512,256]{3,2,1,0:T(8,128)(2,1)} %param.6) | copy-start | bytes 12582916
Sparse Core Ops, SparseCore 0:
  13.6 60.2 reduce-scatter.1
  76.2 20.0 all-reduce.1
where the time goes:
time: 144 us
  waiting for transfers between devices  80.9 us (56%)
  blocking collectives  27.3 us (19%)
  matrix products  15.5 us (11%)
  between operations  13.5 us (9%)
  other arithmetic  5.08 us (4%)
    reduce_scatter x1, waiting for transfers between devices, local(): lax.psum_scatter(partial_value, 'gx', scatter_dimension=1, tiled=True)  60.4 us
    all_gather x1, blocking collectives, local(): gathered = lax.all_gather(gathered, 'gx', axis=1, tiled=True)  22.9 us
    psum x1, waiting for transfers between devices, local(): owned_modes = lax.psum(owned_modes, 'gy')  20.5 us
    dot_general x1, matrix products, local(): jnp.einsum('bnh,hc->bnc', hidden, outer_weight, preferred_element_type=jn...  5.53 us
    all_gather x1, blocking collectives, local(): gathered = lax.all_gather(mixed_modes, 'gy', axis=3, tiled=True)  4.41 us
    another operation x1, other arithmetic  4.14 us
  transfers between devices with their start and end apart: 2, of which 2 were waited for; matrix products, arithmetic and copies ran while one was open for 1% of the time, Pallas kernels for 0%

commit v1 on v0

v1 whole, which is shorter than its diff:
```python
import functools
import math

import jax
import jax.numpy as jnp
from jax import lax
from jax.experimental import pallas as pl
from jax.experimental.pallas import tpu as pltpu
from jax.sharding import PartitionSpec as P


KX = 16
KY = 8
VMEM = pl.BlockSpec(memory_space=pltpu.VMEM)


def hops(mask, low_bits):
    low, high = mask & ((1 << low_bits) - 1), mask >> low_bits
    return low.bit_count() + (high + high.bit_count()) / 2


def share(masks, low_bits):
    order = sorted(masks, key=lambda mask: -hops(mask, low_bits))
    pairs = [(order[at], order[at + 1]) for at in range(0, len(order) - 1, 2)]
    return pairs, order[-1]


def exchange(value, x_masks, y_mask):
    x_devices, y_devices = lax.axis_size("gx"), lax.axis_size("gy")
    pairs = [
        (x * y_devices + y, (x ^ x_masks[x & 1]) * y_devices + (y ^ y_mask))
        for x in range(x_devices)
        for y in range(y_devices)
    ]
    return lax.ppermute(value, ("gx", "gy"), pairs)


def reduce_offsets(x_devices):
    pairs, shared = share(range(1, x_devices // 2), 1)
    keep = []
    for core in (0, 1):
        blocks = [2 * pair[core] + kind for pair in pairs for kind in (0, 1)]
        keep.append(blocks + [2 * shared, 0])
    return [keep[core] + [offset ^ 1 for offset in keep[1 - core]] for core in (0, 1)]


def gather_offsets(x_devices):
    held = [4 * mask for mask in range(x_devices // 4)]
    blocks = [holder ^ (2 * y) ^ offset for holder in (0, 1) for y in (0, 1) for offset in held]
    return [blocks, blocks]


def divide(value, by):
    return value >> (by.bit_length() - 1) if by & (by - 1) == 0 else value // by


def remainder(value, by):
    return value & (by - 1) if by & (by - 1) == 0 else value % by


def write_basis(offsets, own_count, shape, x_wave, y_wave, basis):
    row_count, col_count, total_rows, total_cols = shape
    cells = row_count * col_count
    x_me, y_me = lax.axis_index("gx"), lax.axis_index("gy")
    x_at = divide(lax.broadcasted_iota(jnp.int32, (KX, cells), 1), col_count) + x_me * row_count
    x_turn = remainder(lax.broadcasted_iota(jnp.int32, (KX, cells), 0) * x_at, total_rows)
    x_angle = x_turn.astype(jnp.float32) * (2.0 * math.pi / total_rows)
    x_wave[0], x_wave[1] = jnp.cos(x_angle), jnp.sin(x_angle)
    y_at = remainder(lax.broadcasted_iota(jnp.int32, (KY, cells), 1), col_count) + y_me * col_count
    y_turn = remainder(lax.broadcasted_iota(jnp.int32, (KY, cells), 0) * y_at, total_cols)
    y_angle = y_turn.astype(jnp.float32) * (2.0 * math.pi / total_cols)
    y_wave[0], y_wave[1] = jnp.cos(y_angle), jnp.sin(y_angle)
    run = min(own_count, KY)
    core = x_me & 1
    pending, row = [], 0
    for at in range(len(offsets[0])):
        owner = x_me ^ jnp.where(core == 0, offsets[0][at], offsets[1][at])
        cosines, sines = [], []
        for start in range(0, own_count, run):
            mode = owner * own_count + start
            x_mode = mode // KY
            x_cos, x_sin = x_wave[0, pl.ds(x_mode, 1), :], x_wave[1, pl.ds(x_mode, 1), :]
            if run == KY:
                y_cos, y_sin = y_wave[0], y_wave[1]
            else:
                y_cos, y_sin = y_wave[0, :run], y_wave[1, :run]
                for other in range(run, KY, run):
                    here = mode % KY == other
                    y_cos = jnp.where(here, y_wave[0, other : other + run], y_cos)
                    y_sin = jnp.where(here, y_wave[1, other : other + run], y_sin)
            cosines.append(x_cos * y_cos - x_sin * y_sin)
            sines.append(-(x_sin * y_cos + x_cos * y_sin))
        pending += cosines + sines
        count = sum(piece.shape[0] for piece in pending)
        if count % 16 == 0:
            basis[row : row + count, :] = jnp.concatenate(pending, axis=0).astype(jnp.bfloat16)
            pending, row = [], row + count


def basis_kernel(offsets, own_count, shape, basis, x_wave, y_wave):
    write_basis(offsets, own_count, shape, x_wave, y_wave, basis)


def forward_kernel(basis, field, keep, send):
    half = basis.shape[0] // 2
    for b in range(field.shape[0]):
        send[b] = jnp.dot(basis[half:, :], field[b], preferred_element_type=jnp.float32).astype(jnp.bfloat16)
        keep[b] = jnp.dot(basis[:half, :], field[b], preferred_element_type=jnp.float32)


def skip_kernel(offsets, own_count, shape, field, skip_weight, skip, turned, x_wave, y_wave, basis):
    for b in range(field.shape[0]):
        skip[b] = jnp.dot(field[b], skip_weight[...], preferred_element_type=jnp.float32)
    write_basis(offsets, own_count, shape, x_wave, y_wave, basis)
    turned[...] = basis[...].T


def mix_kernel(scale, own_count, total, other, weight, mixed):
    micro_count, rows, width_count = total.shape
    spectrum = ((total[...] + other[...].astype(jnp.float32)) * scale).reshape(micro_count * rows, width_count)
    mode = remainder(lax.broadcasted_iota(jnp.int32, spectrum.shape, 0), own_count)
    apart = [jnp.where(mode == at, spectrum, 0.0).astype(jnp.bfloat16) for at in range(own_count)]
    apart = jnp.concatenate(apart, axis=1)
    part_width = mixed.shape[-1]
    by = []
    for kind in (0, 1):
        columns = weight[:, kind].reshape(own_count * width_count, part_width)
        product = jnp.dot(apart, columns, preferred_element_type=jnp.float32)
        by.append(product.reshape(micro_count, rows, part_width))
    real = by[0][:, :own_count] - by[1][:, own_count:]
    imaginary = by[1][:, :own_count] + by[0][:, own_count:]
    mixed[...] = jnp.concatenate([real, imaginary], axis=1).astype(jnp.bfloat16)


def gelu(value):
    inner = value * (math.sqrt(2.0 / math.pi) + (math.sqrt(2.0 / math.pi) * 0.044715) * (value * value))
    half = 0.5 * value
    return half + half * jnp.tanh(inner)


def output_kernel(
    scale, tile, chunk, y_devices, mine, theirs, skip, turned, inner_weight, outer_weight, out, modes
):
    micro_count, cells, _ = skip.shape
    step = pl.program_id(0)
    tiles = cells // tile

    @pl.when(step == 0)
    def _():
        y_me = lax.axis_index("gy") if y_devices > 1 else 0
        planes, held_count, _, rows, part_width = mine.shape
        row = 0
        for source in (mine, theirs):
            for y in range(planes // y_devices):
                for part in range(y_devices):
                    plane = y * y_devices + (y_me ^ part)
                    for at in range(held_count):
                        for b in range(micro_count):
                            modes[b, row + at * rows : row + (at + 1) * rows, part * part_width : (part + 1) * part_width] = (
                                source[plane, at, b]
                            )
                row += held_count * rows

    b, start = step // tiles, pl.multiple_of((step % tiles) * tile, tile)
    spectral = jnp.dot(turned[pl.ds(start, tile), :], modes[b], preferred_element_type=jnp.float32)
    active = gelu(spectral * scale + skip[b, pl.ds(start, tile), :]).astype(jnp.bfloat16)

    def inner(at):
        columns = inner_weight[at * chunk : (at + 1) * chunk, :]
        return lax.dot_general(active, columns, (((1,), (1,)), ((), ())), preferred_element_type=jnp.float32)

    chunks = inner_weight.shape[0] // chunk
    total, following = active.astype(jnp.float32), inner(0)
    for at in range(chunks):
        hidden = following
        if at + 1 < chunks:
            following = inner(at + 1)
        rows = outer_weight[at * chunk : (at + 1) * chunk, :]
        total = total + jnp.dot(gelu(hidden).astype(jnp.bfloat16), rows, preferred_element_type=jnp.float32)
    out[0] = total.astype(jnp.bfloat16)


def local(grid_field, spectral_weight, skip_weight, inner_weight, outer_weight):
    micro_count, row_count, col_count, width_count = grid_field.shape
    x_devices = lax.axis_size("gx")
    y_devices = lax.axis_size("gy")
    total_rows = row_count * x_devices
    total_cols = col_count * y_devices
    mode_count = KX * KY
    own_count = mode_count // x_devices
    cells = row_count * col_count
    shape = (row_count, col_count, total_rows, total_cols)
    flat_rows = grid_field.reshape(micro_count, cells, width_count)
    waves = [pltpu.VMEM((2, KX, cells), jnp.float32), pltpu.VMEM((2, KY, cells), jnp.float32)]
    basis_shape = (2 * mode_count, cells)
    matmul = 2 * micro_count * cells * width_count

    basis = pl.pallas_call(
        functools.partial(basis_kernel, reduce_offsets(x_devices), own_count, shape),
        out_shape=jax.ShapeDtypeStruct(basis_shape, jnp.bfloat16),
        out_specs=VMEM,
        scratch_shapes=waves,
        compiler_params=pltpu.CompilerParams(vmem_limit_bytes=16 * 2**20),
        cost_estimate=pl.CostEstimate(flops=8 * matmul * 2 * mode_count, bytes_accessed=2 * flat_rows.size, transcendentals=0),
        name="basis",
    )()
    keep, send = pl.pallas_call(
        forward_kernel,
        out_shape=[
            jax.ShapeDtypeStruct((micro_count, mode_count, width_count), jnp.float32),
            jax.ShapeDtypeStruct((micro_count, mode_count, width_count), jnp.bfloat16),
        ],
        in_specs=[VMEM, VMEM],
        out_specs=[VMEM, VMEM],
        compiler_params=pltpu.CompilerParams(vmem_limit_bytes=16 * 2**20),
        cost_estimate=pl.CostEstimate(flops=8 * matmul * 2 * mode_count, bytes_accessed=2 * flat_rows.size, transcendentals=0),
        name="forward",
    )(basis, flat_rows)

    skip, turned = pl.pallas_call(
        functools.partial(skip_kernel, gather_offsets(x_devices), own_count, shape),
        out_shape=[
            jax.ShapeDtypeStruct((micro_count, cells, width_count), jnp.float32),
            jax.ShapeDtypeStruct((cells, 2 * mode_count), jnp.bfloat16),
        ],
        in_specs=[VMEM, VMEM],
        out_specs=[VMEM, VMEM],
        scratch_shapes=waves + [pltpu.VMEM(basis_shape, jnp.bfloat16)],
        compiler_params=pltpu.CompilerParams(vmem_limit_bytes=16 * 2**20),
        cost_estimate=pl.CostEstimate(flops=matmul * width_count, bytes_accessed=2 * flat_rows.size, transcendentals=0),
        name="skip",
    )(flat_rows, skip_weight)

    def as_blocks(array):
        return array.reshape(micro_count, x_devices // 2, 2 * own_count, width_count)

    pairs, shared = share(range(1, x_devices // 2), 1)
    blocks = as_blocks(keep) + as_blocks(exchange(send, (1, 1), 0)).astype(jnp.float32)
    arrived = [
        exchange(blocks[:, 2 * at : 2 * at + 2].astype(jnp.bfloat16), (2 * pair[0], 2 * pair[1]), 0)
        for at, pair in enumerate(pairs)
    ]
    shared_arrived = exchange(blocks[:, -2].astype(jnp.bfloat16), (2 * shared, 2 * shared), 0)
    summed = sum(piece.astype(jnp.float32) for piece in arrived)
    swapped = exchange(summed[:, 1].astype(jnp.bfloat16), (1, 1), 0)
    total = blocks[:, -1] + summed[:, 0] + shared_arrived.astype(jnp.float32) + swapped.astype(jnp.float32)
    for bit in range(y_devices.bit_length() - 1):
        if bit > 0:
            total = total + other.astype(jnp.float32)
        other = exchange(total.astype(jnp.bfloat16), (0, 0), 1 << bit)

    part_width = spectral_weight.shape[-1]
    mixed = pl.pallas_call(
        functools.partial(mix_kernel, 1.0 / math.sqrt(total_rows * total_cols), own_count),
        out_shape=jax.ShapeDtypeStruct((micro_count, 2 * own_count, part_width), jnp.bfloat16),
        in_specs=[VMEM] * 3,
        out_specs=VMEM,
        compiler_params=pltpu.CompilerParams(vmem_limit_bytes=16 * 2**20),
        cost_estimate=pl.CostEstimate(flops=8 * spectral_weight.size, bytes_accessed=2 * spectral_weight.size, transcendentals=0),
        name="mix",
    )(total, other, spectral_weight)[None]

    pairs, shared = share(range(1, x_devices // 4), 0)
    along = []
    for mask in range(1, x_devices // 4):
        along.append(exchange(mixed, (4 * mask, 4 * mask), 0))
    held = jnp.concatenate([mixed] + along, axis=0)
    plane = [(y, part) for y in (0, 1) for part in range(y_devices)]
    mine = jnp.stack([held] + [exchange(held, (2 * y, 2 * y), part) for y, part in plane[1:]])
    theirs = exchange(mine, (1, 1), 0)

    rows = 2 * own_count
    if rows % 16 or part_width % 128:
        whole = jnp.stack([mine, theirs]).reshape((2, 2, y_devices) + mine.shape[1:])
        whole = jnp.take(whole, lax.axis_index("gy") ^ jnp.arange(y_devices, dtype=jnp.int32), axis=2)
        whole = whole.transpose(0, 1, 4, 3, 5, 2, 6).reshape(2, 2, 1, micro_count, -1, width_count)
        mine, theirs = whole[0], whole[1]
        parts = 1
    else:
        parts = y_devices
    tile = cells
    layer_out = pl.pallas_call(
        functools.partial(output_kernel, 1.0 / math.sqrt(mode_count), tile, inner_weight.shape[0] // 2, parts),
        out_shape=jax.ShapeDtypeStruct((micro_count, cells, width_count), jnp.bfloat16),
        grid=(micro_count * cells // tile,),
        in_specs=[VMEM] * 6,
        out_specs=pl.BlockSpec((1, tile, width_count), lambda i: (i // (cells // tile), i % (cells // tile), 0)),
        scratch_shapes=[
            pltpu.VMEM((micro_count, 2 * mode_count, width_count), jnp.bfloat16),
        ],
        compiler_params=pltpu.CompilerParams(vmem_limit_bytes=32 * 2**20),
        cost_estimate=pl.CostEstimate(
            flops=matmul * (2 * mode_count + 2 * inner_weight.shape[0]), bytes_accessed=4 * flat_rows.size, transcendentals=0
        ),
        name="output",
    )(mine, theirs, skip, turned, inner_weight, outer_weight)
    return layer_out.reshape(micro_count, row_count, col_count, width_count)


def solution(mesh):
    in_specs = (P(None, "gx", "gy", None), P("gx", None, None, "gy"), P(), P(), P())
    out_specs = P(None, "gx", "gy", None)
    return jax.shard_map(local, mesh=mesh, in_specs=in_specs, out_specs=out_specs, check_vma=False)
```

time: 144 us -> 42.2 us (0.29)
  waiting for transfers between devices: 80.9 us -> 14.5 us
  blocking collectives: 27.3 us -> 0 us
  starting transfers between devices: 0.04 us -> 19.7 us
  matrix products: 15.5 us -> 0 us
  between operations: 13.5 us -> 0.13 us
  Pallas kernels: 0 us -> 6.51 us
  other arithmetic: 5.08 us -> 0.16 us
    reduce_scatter x1 -> x0, waiting for transfers between devices: 60.4 us -> none  [local(): lax.psum_scatter(partial_value, 'gx', scatter_dimension=1, tiled=True)]
    all_gather x2 -> x0, blocking collectives: 27.3 us -> none  [the longest x1 22.9 us: local(): gathered = lax.all_gather(gathered, 'gx', axis=1, tiled=True)]
    psum x1 -> x0, waiting for transfers between devices: 20.5 us -> none  [local(): owned_modes = lax.psum(owned_modes, 'gy')]
    ppermute x0 -> x14, starting transfers between devices: none -> 19.7 us  [exchange(): return lax.ppermute(value, ('gx', 'gy'), pairs)]
    dot_general x8 -> x0, matrix products: 15.5 us -> none  [the longest x1 5.53 us: local(): jnp.einsum('bnh,hc->bnc', hidden, outer_weight, preferred_element_type=jn...]
    ppermute x0 -> x14, waiting for transfers between devices: none -> 14.5 us  [exchange(): return lax.ppermute(value, ('gx', 'gy'), pairs)]
    pallas_call x0 -> x5, Pallas kernels: none -> 6.51 us  [the longest x1 4.25 us: local(): pl.pallas_call(functools.partial(output_kernel, 1.0 / math.sqrt(mode_coun...]
    another operation x2, other arithmetic: 4.17 us -> 0.05 us  [local(): jnp.stack([held] + [exchange(held, (2 * y, 2 * y), part) for y, part in p...]
  transfers between devices with their start and end apart: 2 -> 14, of which waited for: 2 -> 12; matrix products, arithmetic and copies ran while one was open for 1% -> 0% of each run, Pallas kernels for 0% -> 2%
where the time goes in v1:
time: 42.2 us; the launch traced here: 42 us
  starting transfers between devices  19.7 us (47%)
  waiting for transfers between devices  14.5 us (34%)
  Pallas kernels  6.51 us (15%)
  local copies, waits for them, and re-layouts  1.02 us (2%)
    ppermute x14, starting transfers between devices, exchange(): return lax.ppermute(value, ('gx', 'gy'), pairs)  19.7 us
    ppermute x14, waiting for transfers between devices, exchange(): return lax.ppermute(value, ('gx', 'gy'), pairs)  14.5 us
    pallas_call x1, Pallas kernels, local(): pl.pallas_call(functools.partial(output_kernel, 1.0 / math.sqrt(mode_coun...  4.25 us
    unnamed x10, local copies, waits for them, and re-layouts  0.98 us
  transfers between devices with their start and end apart: 14, of which 12 were waited for; matrix products, arithmetic and copies ran while one was open for 0% of the time, Pallas kernels for 2%

profile of v1, /device:TPU:0, one launch (start us, length us, event | category | flops | bytes accessed | tf_op | source)
XLA Modules:
  0.0 42.0 jit_solution(6527649018488655016)
XLA Ops:
  0.0 0.0 copy-start.1
  0.0 0.3 basis.1
  0.3 1.0 %copy-done.1 = bf16[2,16,32,512]{3,2,1,0:T(8,128)(2,1)S(1)} copy-done((bf16[2,16,32,512]{3,2,1,0:T(8,128)(2,1)S(1)}, bf16[2,16,32,512]{3,2,1,0:T(8,128)(2,1)}, u32[]{:S(2)}) %copy-start.1) | copy-done | bytes 1048600
  1.2 0.0 copy-start
  1.2 0.4 %forward.1 = (f32[2,128,512]{2,1,0:T(8,128)S(1)}, bf16[2,128,512]{2,1,0:T(8,128)(2,1)S(1)}) custom-call(bf16[256,512]{1,0:T(8,128)(2,1)S(1)} %basis.1, bf16[2,512,512]{2,1,0:T(8,128)(2,1)S(1)} %bitcast.24), custom_call_target="tpu_custom_call" | custom-call | flops 2147483648 | bytes 1048576 | tf_op jit(solution)/shard_map/forward/pallas_call | solution.py:207
  1.7 0.0 copy-start.4
  1.7 0.6 %collective-permute-start = (bf16[2,128,512]{2,1,0:T(8,128)(2,1)S(1)}, bf16[2,128,512]{2,1,0:T(8,128)(2,1)S(1)}, u32[]{:S(2)}, u32[]{:S(2)}) collective-permute-start(bf16[2,128,512]{2,1,0:T(8,128)(2,1)S(1)} %get-tuple-element.10), channel_id=1, source_target_pairs={{0,2},{1,3},{2,0},{3,1},{4,6},{5,7},{6,4},{7,5},{8,10},{9,11},{10,... | collective-permute-start | bytes 786440 | tf_op jit(solution)/shard_map/ppermute | solution.py:35
  2.2 1.2 %collective-permute-done = bf16[2,128,512]{2,1,0:T(8,128)(2,1)S(1)} collective-permute-done((bf16[2,128,512]{2,1,0:T(8,128)(2,1)S(1)}, bf16[2,128,512]{2,1,0:T(8,128)(2,1)S(1)}, u32[]{:S(2)}, u32[]{:S(2)}) %collective-permute-start) | collective-permute-done | bytes 262176 | tf_op jit(solution)/shard_map/ppermute | solution.py:35
  3.4 0.1 convert_add_fusion
  3.5 0.0 copy-start.2
  3.5 0.0 copy-start.3
  3.5 6.0 %collective-permute-start.1 = (bf16[2,2,16,512]{3,2,0,1:T(8,128)(2,1)S(1)}, bf16[2,2,16,512]{3,2,0,1:T(8,128)(2,1)S(1)}, u32[]{:S(2)}, u32[]{:S(2)}) collective-permute-start(bf16[2,2,16,512]{3,2,0,1:T(8,128)(2,1)S(1)} %get-tuple-element.15), channel_id=1, source_target_pairs={{0,28},{1,29},{2,22},{3,23},{4,24},{5,25},{6,18},{7,19},{8,20},{9,... | collective-permute-start | bytes 196616 | tf_op jit(solution)/shard_map/ppermute | solution.py:35
  9.5 0.0 collective-permute-start.3
  9.5 1.9 %collective-permute-start.2 = (bf16[2,2,16,512]{3,2,0,1:T(8,128)(2,1)S(1)}, bf16[2,2,16,512]{3,2,0,1:T(8,128)(2,1)S(1)}, u32[]{:S(2)}, u32[]{:S(2)}) collective-permute-start(bf16[2,2,16,512]{3,2,0,1:T(8,128)(2,1)S(1)} %get-tuple-element.17), channel_id=1, source_target_pairs={{0,24},{1,25},{2,14},{3,15},{4,28},{5,29},{6,10},{7,11},{8,16},{9,... | collective-permute-start | bytes 196616 | tf_op jit(solution)/shard_map/ppermute | solution.py:35
  11.4 1.6 %collective-permute-start.4 = (bf16[2,16,512]{2,1,0:T(8,128)(2,1)S(1)}, bf16[2,16,512]{2,1,0:T(8,128)(2,1)S(1)}, u32[]{:S(2)}, u32[]{:S(2)}) collective-permute-start(bf16[2,16,512]{2,1,0:T(8,128)(2,1)S(1)} %slice_bitcast_fusion), channel_id=1, source_target_pairs={{0,8},{1,9},{2,10},{3,11},{4,12},{5,13},{6,14},{7,15},{8,0},{9,1},... | collective-permute-start | bytes 98312 | tf_op jit(solution)/shard_map/ppermute | solution.py:35
  13.0 0.0 collective-permute-done.1
  13.0 1.7 %collective-permute-done.3 = bf16[2,2,16,512]{3,2,0,1:T(8,128)(2,1)S(1)} collective-permute-done((bf16[2,2,16,512]{3,2,0,1:T(8,128)(2,1)S(1)}, bf16[2,2,16,512]{3,2,0,1:T(8,128)(2,1)S(1)}, u32[]{:S(2)}, u32[]{:S(2)}) %collective-permute-start.3) | collective-permute-done | bytes 65568 | tf_op jit(solution)/shard_map/ppermute | solution.py:35
  14.7 1.0 %collective-permute-done.2 = bf16[2,2,16,512]{3,2,0,1:T(8,128)(2,1)S(1)} collective-permute-done((bf16[2,2,16,512]{3,2,0,1:T(8,128)(2,1)S(1)}, bf16[2,2,16,512]{3,2,0,1:T(8,128)(2,1)S(1)}, u32[]{:S(2)}, u32[]{:S(2)}) %collective-permute-start.2) | collective-permute-done | bytes 65568 | tf_op jit(solution)/shard_map/ppermute | solution.py:35
  15.8 0.1 collective-permute-start.5
  15.9 0.2 collective-permute-done.4
  16.0 1.0 %collective-permute-done.5 = bf16[2,16,512]{2,1,0:T(8,128)(2,1)S(1)} collective-permute-done((bf16[2,16,512]{2,1,0:T(8,128)(2,1)S(1)}, bf16[2,16,512]{2,1,0:T(8,128)(2,1)S(1)}, u32[]{:S(2)}, u32[]{:S(2)}) %collective-permute-start.5) | collective-permute-done | bytes 32800 | tf_op jit(solution)/shard_map/ppermute | solution.py:35
  17.1 1.6 %collective-permute-start.6 = (bf16[2,16,512]{2,1,0:T(8,128)(2,1)S(1)}, bf16[2,16,512]{2,1,0:T(8,128)(2,1)S(1)}, u32[]{:S(2)}, u32[]{:S(2)}) collective-permute-start(bf16[2,16,512]{2,1,0:T(8,128)(2,1)S(1)} %get-tuple-element.13), channel_id=1, source_target_pairs={{0,1},{1,0},{2,3},{3,2},{4,5},{5,4},{6,7},{7,6},{8,9},{9,8},{10,11... | collective-permute-start | bytes 98312 | tf_op jit(solution)/shard_map/ppermute | solution.py:35
  18.7 2.4 %collective-permute-done.6.other = bf16[2,16,512]{2,1,0:T(8,128)(2,1)S(1)} collective-permute-done((bf16[2,16,512]{2,1,0:T(8,128)(2,1)S(1)}, bf16[2,16,512]{2,1,0:T(8,128)(2,1)S(1)}, u32[]{:S(2)}, u32[]{:S(2)}) %collective-permute-start.6) | collective-permute-done | bytes 32800 | tf_op jit(solution)/shard_map/ppermute | solution.py:35
  21.1 0.0 copy-done
  21.1 0.8 %mix.1 = bf16[2,16,256]{2,1,0:T(8,128)(2,1)S(1)} custom-call(f32[2,16,512]{2,1,0:T(8,128)S(1)} %get-tuple-element.14.total, bf16[2,16,512]{2,1,0:T(8,128)(2,1)S(1)} %collective-permute-done.6.other, bf16[8,2,512,256]{3,2,1,0:T(8,128)(2,1)S(1)} %copy-done), custom_call_target="tpu_custom_call" | custom-call | flops 16777216 | bytes 4194304 | tf_op jit(solution)/shard_map/mix/pallas_call | solution.py:253
  21.9 2.3 %collective-permute-start.9 = (bf16[1,2,16,256]{3,2,1,0:T(8,128)(2,1)S(1)}, bf16[1,2,16,256]{3,2,1,0:T(8,128)(2,1)S(1)}, u32[]{:S(2)}, u32[]{:S(2)}) collective-permute-start(bf16[1,2,16,256]{3,2,1,0:T(8,128)(2,1)S(1)} %bitcast.20), channel_id=1, source_target_pairs={{0,24},{1,25},{2,26},{3,27},{4,28},{5,29},{6,30},{7,31},{8,16},{9,... | collective-permute-start | bytes 49160 | tf_op jit(solution)/shard_map/ppermute | solution.py:35
  24.3 0.1 collective-permute-start.8
  24.4 2.0 %collective-permute-start.7 = (bf16[1,2,16,256]{3,2,1,0:T(8,128)(2,1)S(1)}, bf16[1,2,16,256]{3,2,1,0:T(8,128)(2,1)S(1)}, u32[]{:S(2)}, u32[]{:S(2)}) collective-permute-start(bf16[1,2,16,256]{3,2,1,0:T(8,128)(2,1)S(1)} %bitcast.22), channel_id=1, source_target_pairs={{0,8},{1,9},{2,10},{3,11},{4,12},{5,13},{6,14},{7,15},{8,0},{9,1},... | collective-permute-start | bytes 49160 | tf_op jit(solution)/shard_map/ppermute | solution.py:35
  26.4 1.1 %collective-permute-done.9 = bf16[1,2,16,256]{3,2,1,0:T(8,128)(2,1)S(1)} collective-permute-done((bf16[1,2,16,256]{3,2,1,0:T(8,128)(2,1)S(1)}, bf16[1,2,16,256]{3,2,1,0:T(8,128)(2,1)S(1)}, u32[]{:S(2)}, u32[]{:S(2)}) %collective-permute-start.9) | collective-permute-done | bytes 16416 | tf_op jit(solution)/shard_map/ppermute | solution.py:35
  27.5 1.4 %collective-permute-done.8 = bf16[1,2,16,256]{3,2,1,0:T(8,128)(2,1)S(1)} collective-permute-done((bf16[1,2,16,256]{3,2,1,0:T(8,128)(2,1)S(1)}, bf16[1,2,16,256]{3,2,1,0:T(8,128)(2,1)S(1)}, u32[]{:S(2)}, u32[]{:S(2)}) %collective-permute-start.8) | collective-permute-done | bytes 16416 | tf_op jit(solution)/shard_map/ppermute | solution.py:35
  28.9 0.0 collective-permute-done.7
  28.9 0.6 %collective-permute-start.11 = (bf16[4,2,16,256]{3,2,1,0:T(8,128)(2,1)S(1)}, bf16[4,2,16,256]{3,2,1,0:T(8,128)(2,1)S(1)}, u32[]{:S(2)}, u32[]{:S(2)}) collective-permute-start(bf16[4,2,16,256]{3,2,1,0:T(8,128)(2,1)S(1)} %get-tuple-element.19), channel_id=1, source_target_pairs={{0,4},{1,5},{2,6},{3,7},{4,0},{5,1},{6,2},{7,3},{8,12},{9,13},{10,... | collective-permute-start | bytes 196616 | tf_op jit(solution)/shard_map/ppermute | solution.py:35
  29.5 1.5 %collective-permute-start.10 = (bf16[4,2,16,256]{3,2,1,0:T(8,128)(2,1)S(1)}, bf16[4,2,16,256]{3,2,1,0:T(8,128)(2,1)S(1)}, u32[]{:S(2)}, u32[]{:S(2)}) collective-permute-start(bf16[4,2,16,256]{3,2,1,0:T(8,128)(2,1)S(1)} %get-tuple-element.19), channel_id=1, source_target_pairs={{0,1},{1,0},{2,3},{3,2},{4,5},{5,4},{6,7},{7,6},{8,9},{9,8},{10,11... | collective-permute-start | bytes 196616 | tf_op jit(solution)/shard_map/ppermute | solution.py:35
  31.0 1.5 %collective-permute-start.12 = (bf16[4,2,16,256]{3,2,1,0:T(8,128)(2,1)S(1)}, bf16[4,2,16,256]{3,2,1,0:T(8,128)(2,1)S(1)}, u32[]{:S(2)}, u32[]{:S(2)}) collective-permute-start(bf16[4,2,16,256]{3,2,1,0:T(8,128)(2,1)S(1)} %get-tuple-element.19), channel_id=1, source_target_pairs={{0,5},{1,4},{2,7},{3,6},{4,1},{5,0},{6,3},{7,2},{8,13},{9,12},{10,... | collective-permute-start | bytes 196616 | tf_op jit(solution)/shard_map/ppermute | solution.py:35
  32.5 0.8 %collective-permute-done.11 = bf16[4,2,16,256]{3,2,1,0:T(8,128)(2,1)S(1)} collective-permute-done((bf16[4,2,16,256]{3,2,1,0:T(8,128)(2,1)S(1)}, bf16[4,2,16,256]{3,2,1,0:T(8,128)(2,1)S(1)}, u32[]{:S(2)}, u32[]{:S(2)}) %collective-permute-start.11) | collective-permute-done | bytes 65568 | tf_op jit(solution)/shard_map/ppermute | solution.py:35
  33.2 0.5 %collective-permute-done.10 = bf16[4,2,16,256]{3,2,1,0:T(8,128)(2,1)S(1)} collective-permute-done((bf16[4,2,16,256]{3,2,1,0:T(8,128)(2,1)S(1)}, bf16[4,2,16,256]{3,2,1,0:T(8,128)(2,1)S(1)}, u32[]{:S(2)}, u32[]{:S(2)}) %collective-permute-start.10) | collective-permute-done | bytes 65568 | tf_op jit(solution)/shard_map/ppermute | solution.py:35
  33.8 2.4 %collective-permute-done.12 = bf16[4,2,16,256]{3,2,1,0:T(8,128)(2,1)S(1)} collective-permute-done((bf16[4,2,16,256]{3,2,1,0:T(8,128)(2,1)S(1)}, bf16[4,2,16,256]{3,2,1,0:T(8,128)(2,1)S(1)}, u32[]{:S(2)}, u32[]{:S(2)}) %collective-permute-start.12) | collective-permute-done | bytes 65568 | tf_op jit(solution)/shard_map/ppermute | solution.py:35
  36.2 0.1 collective-permute-start.13
  36.3 0.0 copy-done.4
  36.3 0.7 %skip.1 = (f32[2,512,512]{2,1,0:T(8,128)S(1)}, bf16[512,256]{1,0:T(8,128)(2,1)S(1)}) custom-call(bf16[2,512,512]{2,1,0:T(8,128)(2,1)S(1)} %bitcast.25, bf16[512,512]{1,0:T(8,128)(2,1)S(1)} %copy-done.4), custom_call_target="tpu_custom_call" | custom-call | flops 536870912 | bytes 1048576 | tf_op jit(solution)/shard_map/skip/pallas_call | solution.py:220
  37.0 0.8 %collective-permute-done.13.theirs = bf16[4,4,2,16,256]{4,3,2,1,0:T(8,128)(2,1)S(1)} collective-permute-done((bf16[4,4,2,16,256]{4,3,2,1,0:T(8,128)(2,1)S(1)}, bf16[4,4,2,16,256]{4,3,2,1,0:T(8,128)(2,1)S(1)}, u32[]{:S(2)}, u32[]{:S(2)}) %collective-permute-start.13) | collective-permute-done | bytes 262176 | tf_op jit(solution)/shard_map/ppermute | solution.py:35
  37.8 0.0 copy-done.2
  37.8 0.0 copy-done.3
  37.8 4.2 %output.1 = bf16[2,512,512]{2,1,0:T(8,128)(2,1)} custom-call(bf16[4,4,2,16,256]{4,3,2,1,0:T(8,128)(2,1)S(1)} %pad_maximum_fusion.mine, bf16[4,4,2,16,256]{4,3,2,1,0:T(8,128)(2,1)S(1)} %collective-permute-done.13.theirs, f32[2,512,512]{2,1,0:T(8,128)S(1)} %get-tuple-element.11.skip, bf16[512,256]{1,0:T(8,128)(2,1)S(1)} %get-tuple-element.12.turned, ...), custom_call_target="tpu_custom_call" | custom-call | flops 2415919104 | bytes 2097152 | tf_op jit(solution)/shard_map/output/pallas_call | solution.py:282
  (7 shorter events, 0.1 us)
Async XLA Ops:
  0.0 1.2 %copy-start.1 = (bf16[2,16,32,512]{3,2,1,0:T(8,128)(2,1)S(1)}, bf16[2,16,32,512]{3,2,1,0:T(8,128)(2,1)}, u32[]{:S(2)}) copy-start(bf16[2,16,32,512]{3,2,1,0:T(8,128)(2,1)} %param.5) | copy-start | bytes 3145732
  1.2 19.9 %copy-start = (bf16[8,2,512,256]{3,2,1,0:T(8,128)(2,1)S(1)}, bf16[8,2,512,256]{3,2,1,0:T(8,128)(2,1)}, u32[]{:S(2)}) copy-start(bf16[8,2,512,256]{3,2,1,0:T(8,128)(2,1)} %weight.1) | copy-start | bytes 12582916
  1.7 34.6 %copy-start.4 = (bf16[512,512]{1,0:T(8,128)(2,1)S(1)}, bf16[512,512]{1,0:T(8,128)(2,1)}, u32[]{:S(2)}) copy-start(bf16[512,512]{1,0:T(8,128)(2,1)} %skip_weight.1) | copy-start | bytes 1572868
  1.7 1.7 %collective-permute-start = (bf16[2,128,512]{2,1,0:T(8,128)(2,1)S(1)}, bf16[2,128,512]{2,1,0:T(8,128)(2,1)S(1)}, u32[]{:S(2)}, u32[]{:S(2)}) collective-permute-start(bf16[2,128,512]{2,1,0:T(8,128)(2,1)S(1)} %get-tuple-element.10), channel_id=1, source_target_pairs={{0,2},{1,3},{2,0},{3,1},{4,6},{5,7},{6,4},{7,5},{8,10},{9,11},{10,... | collective-permute-start | bytes 786440 | tf_op jit(solution)/shard_map/ppermute | solution.py:35
  3.5 34.3 %copy-start.2 = (bf16[1024,512]{1,0:T(8,128)(2,1)S(1)}, bf16[1024,512]{1,0:T(8,128)(2,1)}, u32[]{:S(2)}) copy-start(bf16[1024,512]{1,0:T(8,128)(2,1)} %inner_weight.1) | copy-start | bytes 3145732
  3.5 34.3 %copy-start.3 = (bf16[1024,512]{1,0:T(8,128)(2,1)S(1)}, bf16[1024,512]{1,0:T(8,128)(2,1)}, u32[]{:S(2)}) copy-start(bf16[1024,512]{1,0:T(8,128)(2,1)} %outer_weight.1) | copy-start | bytes 3145732
  3.5 9.5 %collective-permute-start.1 = (bf16[2,2,16,512]{3,2,0,1:T(8,128)(2,1)S(1)}, bf16[2,2,16,512]{3,2,0,1:T(8,128)(2,1)S(1)}, u32[]{:S(2)}, u32[]{:S(2)}) collective-permute-start(bf16[2,2,16,512]{3,2,0,1:T(8,128)(2,1)S(1)} %get-tuple-element.15), channel_id=1, source_target_pairs={{0,28},{1,29},{2,22},{3,23},{4,24},{5,25},{6,18},{7,19},{8,20},{9,... | collective-permute-start | bytes 196616 | tf_op jit(solution)/shard_map/ppermute | solution.py:35
  9.5 5.2 %collective-permute-start.3 = (bf16[2,2,16,512]{3,2,0,1:T(8,128)(2,1)S(1)}, bf16[2,2,16,512]{3,2,0,1:T(8,128)(2,1)S(1)}, u32[]{:S(2)}, u32[]{:S(2)}) collective-permute-start(bf16[2,2,16,512]{3,2,0,1:T(8,128)(2,1)S(1)} %get-tuple-element.16), channel_id=1, source_target_pairs={{0,16},{1,17},{2,6},{3,7},{4,20},{5,21},{6,2},{7,3},{8,24},{9,25},... | collective-permute-start | bytes 196616 | tf_op jit(solution)/shard_map/ppermute | solution.py:35
  9.5 6.2 %collective-permute-start.2 = (bf16[2,2,16,512]{3,2,0,1:T(8,128)(2,1)S(1)}, bf16[2,2,16,512]{3,2,0,1:T(8,128)(2,1)S(1)}, u32[]{:S(2)}, u32[]{:S(2)}) collective-permute-start(bf16[2,2,16,512]{3,2,0,1:T(8,128)(2,1)S(1)} %get-tuple-element.17), channel_id=1, source_target_pairs={{0,24},{1,25},{2,14},{3,15},{4,28},{5,29},{6,10},{7,11},{8,16},{9,... | collective-permute-start | bytes 196616 | tf_op jit(solution)/shard_map/ppermute | solution.py:35
  11.4 4.6 %collective-permute-start.4 = (bf16[2,16,512]{2,1,0:T(8,128)(2,1)S(1)}, bf16[2,16,512]{2,1,0:T(8,128)(2,1)S(1)}, u32[]{:S(2)}, u32[]{:S(2)}) collective-permute-start(bf16[2,16,512]{2,1,0:T(8,128)(2,1)S(1)} %slice_bitcast_fusion), channel_id=1, source_target_pairs={{0,8},{1,9},{2,10},{3,11},{4,12},{5,13},{6,14},{7,15},{8,0},{9,1},... | collective-permute-start | bytes 98312 | tf_op jit(solution)/shard_map/ppermute | solution.py:35
  15.8 1.3 %collective-permute-start.5 = (bf16[2,16,512]{2,1,0:T(8,128)(2,1)S(1)}, bf16[2,16,512]{2,1,0:T(8,128)(2,1)S(1)}, u32[]{:S(2)}, u32[]{:S(2)}) collective-permute-start(bf16[2,16,512]{2,1,0:T(8,128)(2,1)S(1)} %fusion.3), channel_id=1, source_target_pairs={{0,2},{1,3},{2,0},{3,1},{4,6},{5,7},{6,4},{7,5},{8,10},{9,11},{10,... | collective-permute-start | bytes 98312 | tf_op jit(solution)/shard_map/ppermute | solution.py:35
  17.1 4.0 %collective-permute-start.6 = (bf16[2,16,512]{2,1,0:T(8,128)(2,1)S(1)}, bf16[2,16,512]{2,1,0:T(8,128)(2,1)S(1)}, u32[]{:S(2)}, u32[]{:S(2)}) collective-permute-start(bf16[2,16,512]{2,1,0:T(8,128)(2,1)S(1)} %get-tuple-element.13), channel_id=1, source_target_pairs={{0,1},{1,0},{2,3},{3,2},{4,5},{5,4},{6,7},{7,6},{8,9},{9,8},{10,11... | collective-permute-start | bytes 98312 | tf_op jit(solution)/shard_map/ppermute | solution.py:35
  21.9 5.6 %collective-permute-start.9 = (bf16[1,2,16,256]{3,2,1,0:T(8,128)(2,1)S(1)}, bf16[1,2,16,256]{3,2,1,0:T(8,128)(2,1)S(1)}, u32[]{:S(2)}, u32[]{:S(2)}) collective-permute-start(bf16[1,2,16,256]{3,2,1,0:T(8,128)(2,1)S(1)} %bitcast.20), channel_id=1, source_target_pairs={{0,24},{1,25},{2,26},{3,27},{4,28},{5,29},{6,30},{7,31},{8,16},{9,... | collective-permute-start | bytes 49160 | tf_op jit(solution)/shard_map/ppermute | solution.py:35
  24.3 4.6 %collective-permute-start.8 = (bf16[1,2,16,256]{3,2,1,0:T(8,128)(2,1)S(1)}, bf16[1,2,16,256]{3,2,1,0:T(8,128)(2,1)S(1)}, u32[]{:S(2)}, u32[]{:S(2)}) collective-permute-start(bf16[1,2,16,256]{3,2,1,0:T(8,128)(2,1)S(1)} %bitcast.21), channel_id=1, source_target_pairs={{0,16},{1,17},{2,18},{3,19},{4,20},{5,21},{6,22},{7,23},{8,24},{9,... | collective-permute-start | bytes 49160 | tf_op jit(solution)/shard_map/ppermute | solution.py:35
  24.4 4.5 %collective-permute-start.7 = (bf16[1,2,16,256]{3,2,1,0:T(8,128)(2,1)S(1)}, bf16[1,2,16,256]{3,2,1,0:T(8,128)(2,1)S(1)}, u32[]{:S(2)}, u32[]{:S(2)}) collective-permute-start(bf16[1,2,16,256]{3,2,1,0:T(8,128)(2,1)S(1)} %bitcast.22), channel_id=1, source_target_pairs={{0,8},{1,9},{2,10},{3,11},{4,12},{5,13},{6,14},{7,15},{8,0},{9,1},... | collective-permute-start | bytes 49160 | tf_op jit(solution)/shard_map/ppermute | solution.py:35
  28.9 4.3 %collective-permute-start.11 = (bf16[4,2,16,256]{3,2,1,0:T(8,128)(2,1)S(1)}, bf16[4,2,16,256]{3,2,1,0:T(8,128)(2,1)S(1)}, u32[]{:S(2)}, u32[]{:S(2)}) collective-permute-start(bf16[4,2,16,256]{3,2,1,0:T(8,128)(2,1)S(1)} %get-tuple-element.19), channel_id=1, source_target_pairs={{0,4},{1,5},{2,6},{3,7},{4,0},{5,1},{6,2},{7,3},{8,12},{9,13},{10,... | collective-permute-start | bytes 196616 | tf_op jit(solution)/shard_map/ppermute | solution.py:35
  29.5 4.3 %collective-permute-start.10 = (bf16[4,2,16,256]{3,2,1,0:T(8,128)(2,1)S(1)}, bf16[4,2,16,256]{3,2,1,0:T(8,128)(2,1)S(1)}, u32[]{:S(2)}, u32[]{:S(2)}) collective-permute-start(bf16[4,2,16,256]{3,2,1,0:T(8,128)(2,1)S(1)} %get-tuple-element.19), channel_id=1, source_target_pairs={{0,1},{1,0},{2,3},{3,2},{4,5},{5,4},{6,7},{7,6},{8,9},{9,8},{10,11... | collective-permute-start | bytes 196616 | tf_op jit(solution)/shard_map/ppermute | solution.py:35
  31.0 5.2 %collective-permute-start.12 = (bf16[4,2,16,256]{3,2,1,0:T(8,128)(2,1)S(1)}, bf16[4,2,16,256]{3,2,1,0:T(8,128)(2,1)S(1)}, u32[]{:S(2)}, u32[]{:S(2)}) collective-permute-start(bf16[4,2,16,256]{3,2,1,0:T(8,128)(2,1)S(1)} %get-tuple-element.19), channel_id=1, source_target_pairs={{0,5},{1,4},{2,7},{3,6},{4,1},{5,0},{6,3},{7,2},{8,13},{9,12},{10,... | collective-permute-start | bytes 196616 | tf_op jit(solution)/shard_map/ppermute | solution.py:35
  36.2 1.6 %collective-permute-start.13 = (bf16[4,4,2,16,256]{4,3,2,1,0:T(8,128)(2,1)S(1)}, bf16[4,4,2,16,256]{4,3,2,1,0:T(8,128)(2,1)S(1)}, u32[]{:S(2)}, u32[]{:S(2)}) collective-permute-start(bf16[4,4,2,16,256]{4,3,2,1,0:T(8,128)(2,1)S(1)} %pad_maximum_fusion.mine), channel_id=1, source_target_pairs={{0,2},{1,3},{2,0},{3,1},{4,6},{5,7},{6,4},{7,5},{8,10},{9,11},{10,... | collective-permute-start | bytes 786440 | tf_op jit(solution)/shard_map/ppermute | solution.py:35

commit v2 on v1

--- a/solution.py
+++ b/solution.py
@@ -14,21 +14,31 @@
 VMEM = pl.BlockSpec(memory_space=pltpu.VMEM)
 
 
-def hops(mask, low_bits):
-    low, high = mask & ((1 << low_bits) - 1), mask >> low_bits
-    return low.bit_count() + (high + high.bit_count()) / 2
-
-
-def share(masks, low_bits):
-    order = sorted(masks, key=lambda mask: -hops(mask, low_bits))
-    pairs = [(order[at], order[at + 1]) for at in range(0, len(order) - 1, 2)]
-    return pairs, order[-1]
-
-
-def exchange(value, x_masks, y_mask):
+def reduce_peers(chips):
+    even, odd = list(range(chips - 2, 0, -2)), list(range(chips - 1, 1, -2))
+    if not even:
+        return [], 1
+    return list(zip(even[1:] + [1], odd)), even[0]
+
+
+def gather_peers(masks):
+    masks = list(masks)
+    return [(masks[at], masks[at + 1]) for at in range(0, len(masks) - 1, 2)], masks[-1]
+
+
+def along_peers(places):
+    middle = places // 2
+    return gather_peers([mask for mask in range(1, places) if mask != middle] + [middle])
+
+
+def plane_peers(y_devices):
+    return gather_peers([(y, part) for y in (0, 1) for part in range(y_devices) if y or part])
+
+
+def exchange(value, x_masks, y_masks=(0, 0)):
     x_devices, y_devices = lax.axis_size("gx"), lax.axis_size("gy")
     pairs = [
-        (x * y_devices + y, (x ^ x_masks[x & 1]) * y_devices + (y ^ y_mask))
+        (x * y_devices + y, (x ^ x_masks[x & 1]) * y_devices + (y ^ y_masks[x & 1]))
         for x in range(x_devices)
         for y in range(y_devices)
     ]
@@ -36,7 +46,7 @@
 
 
 def reduce_offsets(x_devices):
-    pairs, shared = share(range(1, x_devices // 2), 1)
+    pairs, shared = reduce_peers(x_devices // 2)
     keep = []
     for core in (0, 1):
         blocks = [2 * pair[core] + kind for pair in pairs for kind in (0, 1)]
@@ -45,9 +55,26 @@
 
 
 def gather_offsets(x_devices):
-    held = [4 * mask for mask in range(x_devices // 4)]
-    blocks = [holder ^ (2 * y) ^ offset for holder in (0, 1) for y in (0, 1) for offset in held]
-    return [blocks, blocks]
+    pairs, shared = along_peers(x_devices // 4)
+    held = []
+    for core in (0, 1):
+        held.append([0, 4 * shared] + [4 * pair[core] + kind for pair in pairs for kind in (0, 1)])
+    return [
+        [holder ^ (2 * y) ^ offset for holder in (0, 1) for y in (0, 1) for offset in held[core ^ holder]]
+        for core in (0, 1)
+    ]
+
+
+def find_blocks(y_devices, core, chip, mine, theirs):
+    pairs, shared = plane_peers(y_devices)
+    blocks = {(holder, 0, 0): chip(holder) for holder in (0, 1)}
+    blocks[0, *shared], blocks[1, *shared] = mine(0), theirs(0)
+    for at, pair in enumerate(pairs):
+        for server in (0, 1):
+            for holder in (0, 1):
+                ours, other = mine(1 + 2 * at + holder), theirs(1 + 2 * at + (1 - holder))
+                blocks[holder, *pair[server]] = jnp.where(core == server, ours, other)
+    return blocks
 
 
 def divide(value, by):
@@ -101,11 +128,11 @@
     write_basis(offsets, own_count, shape, x_wave, y_wave, basis)
 
 
-def forward_kernel(basis, field, keep, send):
-    half = basis.shape[0] // 2
+def forward_kernel(half, basis, field, out):
+    rows = out.shape[1]
     for b in range(field.shape[0]):
-        send[b] = jnp.dot(basis[half:, :], field[b], preferred_element_type=jnp.float32).astype(jnp.bfloat16)
-        keep[b] = jnp.dot(basis[:half, :], field[b], preferred_element_type=jnp.float32)
+        product = jnp.dot(basis[half * rows : (half + 1) * rows, :], field[b], preferred_element_type=jnp.float32)
+        out[b] = product.astype(out.dtype)
 
 
 def skip_kernel(offsets, own_count, shape, field, skip_weight, skip, turned, x_wave, y_wave, basis):
@@ -139,7 +166,7 @@
 
 
 def output_kernel(
-    scale, tile, chunk, y_devices, mine, theirs, skip, turned, inner_weight, outer_weight, out, modes
+    scale, tile, chunk, y_devices, chip, mine, theirs, skip, turned, inner_weight, outer_weight, out, modes
 ):
     micro_count, cells, _ = skip.shape
     step = pl.program_id(0)
@@ -147,22 +174,28 @@
 
     @pl.when(step == 0)
     def _():
-        y_me = lax.axis_index("gy") if y_devices > 1 else 0
-        planes, held_count, _, rows, part_width = mine.shape
-        row = 0
-        for source in (mine, theirs):
-            for y in range(planes // y_devices):
-                for part in range(y_devices):
-                    plane = y * y_devices + (y_me ^ part)
-                    for at in range(held_count):
-                        for b in range(micro_count):
-                            modes[b, row + at * rows : row + (at + 1) * rows, part * part_width : (part + 1) * part_width] = (
-                                source[plane, at, b]
-                            )
-                row += held_count * rows
+        if y_devices == 1:
+            count = chip.shape[2]
+            for at in range(chip.shape[0]):
+                for b in range(micro_count):
+                    modes[b, 0, at * count : (at + 1) * count, :] = chip[at, b]
+            return
+        core, y_me = lax.axis_index("gx") & 1, lax.axis_index("gy")
+        _, held_count, _, rows, part_width = chip.shape
+        count = held_count * rows
+        for b in range(micro_count):
+            found = find_blocks(
+                y_devices, core, lambda i: chip[i, :, b], lambda i: mine[i, :, b], lambda i: theirs[i, :, b]
+            )
+            for (holder, y, part), blocks in found.items():
+                at = (2 * holder + y) * count
+                modes[b, y_me ^ part, at : at + count, :] = blocks.reshape(count, part_width)
 
     b, start = step // tiles, pl.multiple_of((step % tiles) * tile, tile)
-    spectral = jnp.dot(turned[pl.ds(start, tile), :], modes[b], preferred_element_type=jnp.float32)
+    waves = turned[pl.ds(start, tile), :]
+    spectral = jnp.concatenate(
+        [jnp.dot(waves, modes[b, part], preferred_element_type=jnp.float32) for part in range(modes.shape[1])], axis=1
+    )
     active = gelu(spectral * scale + skip[b, pl.ds(start, tile), :]).astype(jnp.bfloat16)
 
     def inner(at):
@@ -204,18 +237,22 @@
         cost_estimate=pl.CostEstimate(flops=8 * matmul * 2 * mode_count, bytes_accessed=2 * flat_rows.size, transcendentals=0),
         name="basis",
     )()
-    keep, send = pl.pallas_call(
-        forward_kernel,
-        out_shape=[
-            jax.ShapeDtypeStruct((micro_count, mode_count, width_count), jnp.float32),
-            jax.ShapeDtypeStruct((micro_count, mode_count, width_count), jnp.bfloat16),
-        ],
-        in_specs=[VMEM, VMEM],
-        out_specs=[VMEM, VMEM],
-        compiler_params=pltpu.CompilerParams(vmem_limit_bytes=16 * 2**20),
-        cost_estimate=pl.CostEstimate(flops=8 * matmul * 2 * mode_count, bytes_accessed=2 * flat_rows.size, transcendentals=0),
-        name="forward",
-    )(basis, flat_rows)
+
+    def forward(half, kind):
+        return pl.pallas_call(
+            functools.partial(forward_kernel, half),
+            out_shape=jax.ShapeDtypeStruct((micro_count, mode_count, width_count), kind),
+            in_specs=[VMEM, VMEM],
+            out_specs=VMEM,
+            compiler_params=pltpu.CompilerParams(vmem_limit_bytes=16 * 2**20),
+            cost_estimate=pl.CostEstimate(
+                flops=8 * matmul * mode_count, bytes_accessed=2 * flat_rows.size, transcendentals=0
+            ),
+            name="forward",
+        )(basis, flat_rows)
+
+    send = forward(1, jnp.bfloat16)
+    keep = forward(0, jnp.float32)
 
     skip, turned = pl.pallas_call(
         functools.partial(skip_kernel, gather_offsets(x_devices), own_count, shape),
@@ -234,20 +271,20 @@
     def as_blocks(array):
         return array.reshape(micro_count, x_devices // 2, 2 * own_count, width_count)
 
-    pairs, shared = share(range(1, x_devices // 2), 1)
-    blocks = as_blocks(keep) + as_blocks(exchange(send, (1, 1), 0)).astype(jnp.float32)
-    arrived = [
-        exchange(blocks[:, 2 * at : 2 * at + 2].astype(jnp.bfloat16), (2 * pair[0], 2 * pair[1]), 0)
-        for at, pair in enumerate(pairs)
-    ]
-    shared_arrived = exchange(blocks[:, -2].astype(jnp.bfloat16), (2 * shared, 2 * shared), 0)
+    pairs, shared = reduce_peers(x_devices // 2)
+    sent = exchange(send, (1, 1))
+    blocks = as_blocks(keep) + as_blocks(sent).astype(jnp.float32)
+    arrived = []
+    for at, pair in enumerate(pairs):
+        arrived.append(exchange(blocks[:, 2 * at : 2 * at + 2].astype(jnp.bfloat16), (2 * pair[0], 2 * pair[1])))
+    shared_arrived = exchange(blocks[:, -2].astype(jnp.bfloat16), (2 * shared, 2 * shared))
     summed = sum(piece.astype(jnp.float32) for piece in arrived)
-    swapped = exchange(summed[:, 1].astype(jnp.bfloat16), (1, 1), 0)
+    swapped = exchange(summed[:, 1].astype(jnp.bfloat16), (1, 1))
     total = blocks[:, -1] + summed[:, 0] + shared_arrived.astype(jnp.float32) + swapped.astype(jnp.float32)
     for bit in range(y_devices.bit_length() - 1):
         if bit > 0:
             total = total + other.astype(jnp.float32)
-        other = exchange(total.astype(jnp.bfloat16), (0, 0), 1 << bit)
+        other = exchange(total.astype(jnp.bfloat16), (0, 0), (1 << bit, 1 << bit))
 
     part_width = spectral_weight.shape[-1]
     mixed = pl.pallas_call(
@@ -260,40 +297,50 @@
         name="mix",
     )(total, other, spectral_weight)[None]
 
-    pairs, shared = share(range(1, x_devices // 4), 0)
+    pairs, shared = along_peers(x_devices // 4)
+    sibling = exchange(mixed, (1, 1))
+    shared_along = exchange(mixed, (4 * shared, 4 * shared))
+    chip = jnp.concatenate([mixed, sibling])
     along = []
-    for mask in range(1, x_devices // 4):
-        along.append(exchange(mixed, (4 * mask, 4 * mask), 0))
-    held = jnp.concatenate([mixed] + along, axis=0)
-    plane = [(y, part) for y in (0, 1) for part in range(y_devices)]
-    mine = jnp.stack([held] + [exchange(held, (2 * y, 2 * y), part) for y, part in plane[1:]])
-    theirs = exchange(mine, (1, 1), 0)
+    for pair in pairs:
+        along.append(exchange(chip, (4 * pair[0], 4 * pair[1])))
+    held = jnp.concatenate([mixed, shared_along] + along)
+
+    pairs, shared = plane_peers(y_devices)
+    sibling = exchange(held, (1, 1))
+    shared_plane = exchange(held, (2 * shared[0], 2 * shared[0]), (shared[1], shared[1]))
+    chip = jnp.stack([held, sibling])
+    planes = []
+    for one, two in pairs:
+        planes.append(exchange(chip, (2 * one[0], 2 * two[0]), (one[1], two[1])))
+    mine = jnp.concatenate([shared_plane[None]] + planes)
+    theirs = exchange(mine, (1, 1))
 
     rows = 2 * own_count
+    parts = y_devices
     if rows % 16 or part_width % 128:
-        whole = jnp.stack([mine, theirs]).reshape((2, 2, y_devices) + mine.shape[1:])
-        whole = jnp.take(whole, lax.axis_index("gy") ^ jnp.arange(y_devices, dtype=jnp.int32), axis=2)
-        whole = whole.transpose(0, 1, 4, 3, 5, 2, 6).reshape(2, 2, 1, micro_count, -1, width_count)
-        mine, theirs = whole[0], whole[1]
-        parts = 1
-    else:
-        parts = y_devices
+        core = lax.axis_index("gx") & 1
+        found = find_blocks(y_devices, core, lambda i: chip[i], lambda i: mine[i], lambda i: theirs[i])
+        whole = jnp.stack([jnp.stack([found[h, y, p] for p in range(y_devices)]) for h in (0, 1) for y in (0, 1)])
+        whole = jnp.take(whole, lax.axis_index("gy") ^ jnp.arange(y_devices, dtype=jnp.int32), axis=1)
+        chip = whole.transpose(0, 3, 2, 4, 1, 5).reshape(4, micro_count, -1, width_count)
+        parts, mine, theirs = 1, chip[:, :1, :16], chip[:, :1, :16]
     tile = cells
     layer_out = pl.pallas_call(
         functools.partial(output_kernel, 1.0 / math.sqrt(mode_count), tile, inner_weight.shape[0] // 2, parts),
         out_shape=jax.ShapeDtypeStruct((micro_count, cells, width_count), jnp.bfloat16),
         grid=(micro_count * cells // tile,),
-        in_specs=[VMEM] * 6,
+        in_specs=[VMEM] * 7,
         out_specs=pl.BlockSpec((1, tile, width_count), lambda i: (i // (cells // tile), i % (cells // tile), 0)),
         scratch_shapes=[
-            pltpu.VMEM((micro_count, 2 * mode_count, width_count), jnp.bfloat16),
+            pltpu.VMEM((micro_count, parts, 2 * mode_count, width_count // parts), jnp.bfloat16),
         ],
         compiler_params=pltpu.CompilerParams(vmem_limit_bytes=32 * 2**20),
         cost_estimate=pl.CostEstimate(
             flops=matmul * (2 * mode_count + 2 * inner_weight.shape[0]), bytes_accessed=4 * flat_rows.size, transcendentals=0
         ),
         name="output",
-    )(mine, theirs, skip, turned, inner_weight, outer_weight)
+    )(chip, mine, theirs, skip, turned, inner_weight, outer_weight)
     return layer_out.reshape(micro_count, row_count, col_count, width_count)
 
 

time: 42.2 us -> 42.4 us (level)
  starting transfers between devices: 19.7 us -> 16 us
  waiting for transfers between devices: 14.5 us -> 18.2 us
    ppermute x14, starting transfers between devices: 19.7 us -> 16 us  [exchange(): return lax.ppermute(value, ('gx', 'gy'), pairs)]
    ppermute x14, waiting for transfers between devices: 14.5 us -> 18.2 us  [exchange(): return lax.ppermute(value, ('gx', 'gy'), pairs)]
  transfers between devices with their start and end apart: 14 -> 14, of which waited for: 12 -> 10; matrix products, arithmetic and copies ran while one was open for 0% -> 0% of each run, Pallas kernels for 2% -> 2%
where the time goes in v2:
time: 42.4 us; the launch traced here: 42.2 us
  waiting for transfers between devices  18.2 us (43%)
  starting transfers between devices  16 us (38%)
  Pallas kernels  6.67 us (16%)
  local copies, waits for them, and re-layouts  1.02 us (2%)
    ppermute x14, waiting for transfers between devices, exchange(): return lax.ppermute(value, ('gx', 'gy'), pairs)  18.2 us
    ppermute x14, starting transfers between devices, exchange(): return lax.ppermute(value, ('gx', 'gy'), pairs)  16 us
    pallas_call x1, Pallas kernels, local(): pl.pallas_call(functools.partial(output_kernel, 1.0 / math.sqrt(mode_coun...  4.25 us
    unnamed x10, local copies, waits for them, and re-layouts  0.98 us
  transfers between devices with their start and end apart: 14, of which 10 were waited for; matrix products, arithmetic and copies ran while one was open for 0% of the time, Pallas kernels for 2%

profile of v2, /device:TPU:0, one launch (start us, length us, event | category | flops | bytes accessed | tf_op | source)
XLA Modules:
  0.0 42.2 jit_solution(9844460511340076734)
XLA Ops:
  0.0 0.0 copy-start.1
  0.0 0.3 basis.1
  0.3 1.0 %copy-done.1 = bf16[2,16,32,512]{3,2,1,0:T(8,128)(2,1)S(1)} copy-done((bf16[2,16,32,512]{3,2,1,0:T(8,128)(2,1)S(1)}, bf16[2,16,32,512]{3,2,1,0:T(8,128)(2,1)}, u32[]{:S(2)}) %copy-start.1) | copy-done | bytes 1048600
  1.2 0.3 forward.3
  1.5 0.0 copy-start
  1.5 0.6 %collective-permute-start = (bf16[2,128,512]{2,1,0:T(8,128)(2,1)S(1)}, bf16[2,128,512]{2,1,0:T(8,128)(2,1)S(1)}, u32[]{:S(2)}, u32[]{:S(2)}) collective-permute-start(bf16[2,128,512]{2,1,0:T(8,128)(2,1)S(1)} %forward.3), channel_id=1, source_target_pairs={{0,2},{1,3},{2,0},{3,1},{4,6},{5,7},{6,4},{7,5},{8,10},{9,11},{10,... | collective-permute-start | bytes 786440 | tf_op jit(solution)/shard_map/ppermute | solution.py:45
  2.1 0.3 forward.2
  2.4 0.0 copy-start.4
  2.4 0.8 %collective-permute-done = bf16[2,128,512]{2,1,0:T(8,128)(2,1)S(1)} collective-permute-done((bf16[2,128,512]{2,1,0:T(8,128)(2,1)S(1)}, bf16[2,128,512]{2,1,0:T(8,128)(2,1)S(1)}, u32[]{:S(2)}, u32[]{:S(2)}) %collective-permute-start) | collective-permute-done | bytes 262176 | tf_op jit(solution)/shard_map/ppermute | solution.py:45
  3.3 0.1 convert_add_fusion
  3.3 0.0 copy-start.2
  3.4 0.0 copy-start.3
  3.4 4.0 %collective-permute-start.1 = (bf16[2,2,16,512]{3,2,0,1:T(8,128)(2,1)S(1)}, bf16[2,2,16,512]{3,2,0,1:T(8,128)(2,1)S(1)}, u32[]{:S(2)}, u32[]{:S(2)}) collective-permute-start(bf16[2,2,16,512]{3,2,0,1:T(8,128)(2,1)S(1)} %get-tuple-element.11), channel_id=1, source_target_pairs={{0,16},{1,17},{2,30},{3,31},{4,20},{5,21},{6,26},{7,27},{8,24},{9,... | collective-permute-start | bytes 196616 | tf_op jit(solution)/shard_map/ppermute | solution.py:45
  7.4 1.5 %collective-permute-start.3 = (bf16[2,2,16,512]{3,2,0,1:T(8,128)(2,1)S(1)}, bf16[2,2,16,512]{3,2,0,1:T(8,128)(2,1)S(1)}, u32[]{:S(2)}, u32[]{:S(2)}) collective-permute-start(bf16[2,2,16,512]{3,2,0,1:T(8,128)(2,1)S(1)} %get-tuple-element.12), channel_id=1, source_target_pairs={{0,4},{1,5},{2,14},{3,15},{4,0},{5,1},{6,10},{7,11},{8,12},{9,13},... | collective-permute-start | bytes 196616 | tf_op jit(solution)/shard_map/ppermute | solution.py:45
  8.9 1.6 %collective-permute-start.2 = (bf16[2,2,16,512]{3,2,0,1:T(8,128)(2,1)S(1)}, bf16[2,2,16,512]{3,2,0,1:T(8,128)(2,1)S(1)}, u32[]{:S(2)}, u32[]{:S(2)}) collective-permute-start(bf16[2,2,16,512]{3,2,0,1:T(8,128)(2,1)S(1)} %get-tuple-element.13), channel_id=1, source_target_pairs={{0,8},{1,9},{2,22},{3,23},{4,12},{5,13},{6,18},{7,19},{8,0},{9,1},... | collective-permute-start | bytes 196616 | tf_op jit(solution)/shard_map/ppermute | solution.py:45
  10.5 0.2 collective-permute-start.4
  10.7 0.0 collective-permute-done.1
  10.8 1.1 %collective-permute-done.3 = bf16[2,2,16,512]{3,2,0,1:T(8,128)(2,1)S(1)} collective-permute-done((bf16[2,2,16,512]{3,2,0,1:T(8,128)(2,1)S(1)}, bf16[2,2,16,512]{3,2,0,1:T(8,128)(2,1)S(1)}, u32[]{:S(2)}, u32[]{:S(2)}) %collective-permute-start.3) | collective-permute-done | bytes 65568 | tf_op jit(solution)/shard_map/ppermute | solution.py:45
  11.9 2.0 %collective-permute-done.2 = bf16[2,2,16,512]{3,2,0,1:T(8,128)(2,1)S(1)} collective-permute-done((bf16[2,2,16,512]{3,2,0,1:T(8,128)(2,1)S(1)}, bf16[2,2,16,512]{3,2,0,1:T(8,128)(2,1)S(1)}, u32[]{:S(2)}, u32[]{:S(2)}) %collective-permute-start.2) | collective-permute-done | bytes 65568 | tf_op jit(solution)/shard_map/ppermute | solution.py:45
  14.0 0.7 %collective-permute-start.5 = (bf16[2,16,512]{2,1,0:T(8,128)(2,1)S(1)}, bf16[2,16,512]{2,1,0:T(8,128)(2,1)S(1)}, u32[]{:S(2)}, u32[]{:S(2)}) collective-permute-start(bf16[2,16,512]{2,1,0:T(8,128)(2,1)S(1)} %fusion.3), channel_id=1, source_target_pairs={{0,2},{1,3},{2,0},{3,1},{4,6},{5,7},{6,4},{7,5},{8,10},{9,11},{10,... | collective-permute-start | bytes 98312 | tf_op jit(solution)/shard_map/ppermute | solution.py:45
  14.6 1.6 %collective-permute-done.4 = bf16[2,16,512]{2,1,0:T(8,128)(2,1)S(1)} collective-permute-done((bf16[2,16,512]{2,1,0:T(8,128)(2,1)S(1)}, bf16[2,16,512]{2,1,0:T(8,128)(2,1)S(1)}, u32[]{:S(2)}, u32[]{:S(2)}) %collective-permute-start.4) | collective-permute-done | bytes 32800 | tf_op jit(solution)/shard_map/ppermute | solution.py:45
  16.2 0.0 collective-permute-done.5
  16.3 1.6 %collective-permute-start.6 = (bf16[2,16,512]{2,1,0:T(8,128)(2,1)S(1)}, bf16[2,16,512]{2,1,0:T(8,128)(2,1)S(1)}, u32[]{:S(2)}, u32[]{:S(2)}) collective-permute-start(bf16[2,16,512]{2,1,0:T(8,128)(2,1)S(1)} %get-tuple-element.9), channel_id=1, source_target_pairs={{0,1},{1,0},{2,3},{3,2},{4,5},{5,4},{6,7},{7,6},{8,9},{9,8},{10,11... | collective-permute-start | bytes 98312 | tf_op jit(solution)/shard_map/ppermute | solution.py:45
  17.8 2.4 %collective-permute-done.6.other = bf16[2,16,512]{2,1,0:T(8,128)(2,1)S(1)} collective-permute-done((bf16[2,16,512]{2,1,0:T(8,128)(2,1)S(1)}, bf16[2,16,512]{2,1,0:T(8,128)(2,1)S(1)}, u32[]{:S(2)}, u32[]{:S(2)}) %collective-permute-start.6) | collective-permute-done | bytes 32800 | tf_op jit(solution)/shard_map/ppermute | solution.py:45
  20.2 0.0 copy-done
  20.2 0.8 %mix.1 = bf16[2,16,256]{2,1,0:T(8,128)(2,1)S(1)} custom-call(f32[2,16,512]{2,1,0:T(8,128)S(1)} %get-tuple-element.10.total, bf16[2,16,512]{2,1,0:T(8,128)(2,1)S(1)} %collective-permute-done.6.other, bf16[8,2,512,256]{3,2,1,0:T(8,128)(2,1)S(1)} %copy-done), custom_call_target="tpu_custom_call" | custom-call | flops 16777216 | bytes 4194304 | tf_op jit(solution)/shard_map/mix/pallas_call | solution.py:290
  21.1 0.1 collective-permute-start.8
  21.1 1.2 %collective-permute-done.8 = bf16[1,2,16,256]{3,2,1,0:T(8,128)(2,1)S(1)} collective-permute-done((bf16[1,2,16,256]{3,2,1,0:T(8,128)(2,1)S(1)}, bf16[1,2,16,256]{3,2,1,0:T(8,128)(2,1)S(1)}, u32[]{:S(2)}, u32[]{:S(2)}) %collective-permute-start.8) | collective-permute-done | bytes 16416 | tf_op jit(solution)/shard_map/ppermute | solution.py:45
  22.3 0.7 %collective-permute-start.9 = (bf16[2,2,16,256]{3,2,1,0:T(8,128)(2,1)S(1)}, bf16[2,2,16,256]{3,2,1,0:T(8,128)(2,1)S(1)}, u32[]{:S(2)}, u32[]{:S(2)}) collective-permute-start(bf16[2,2,16,256]{3,2,1,0:T(8,128)(2,1)S(1)} %pad_maximum_fusion.3), channel_id=1, source_target_pairs={{0,8},{1,9},{2,26},{3,27},{4,12},{5,13},{6,30},{7,31},{8,0},{9,1},... | collective-permute-start | bytes 98312 | tf_op jit(solution)/shard_map/ppermute | solution.py:45
  23.0 1.8 %collective-permute-start.7 = (bf16[1,2,16,256]{3,2,1,0:T(8,128)(2,1)S(1)}, bf16[1,2,16,256]{3,2,1,0:T(8,128)(2,1)S(1)}, u32[]{:S(2)}, u32[]{:S(2)}) collective-permute-start(bf16[1,2,16,256]{3,2,1,0:T(8,128)(2,1)S(1)} %bitcast.21), channel_id=1, source_target_pairs={{0,16},{1,17},{2,18},{3,19},{4,20},{5,21},{6,22},{7,23},{8,24},{9,... | collective-permute-start | bytes 49160 | tf_op jit(solution)/shard_map/ppermute | solution.py:45
  24.8 2.8 %collective-permute-done.7 = bf16[1,2,16,256]{3,2,1,0:T(8,128)(2,1)S(1)} collective-permute-done((bf16[1,2,16,256]{3,2,1,0:T(8,128)(2,1)S(1)}, bf16[1,2,16,256]{3,2,1,0:T(8,128)(2,1)S(1)}, u32[]{:S(2)}, u32[]{:S(2)}) %collective-permute-start.7) | collective-permute-done | bytes 16416 | tf_op jit(solution)/shard_map/ppermute | solution.py:45
  27.7 0.0 collective-permute-done.9
  27.7 0.2 collective-permute-start.10
  27.9 1.1 %collective-permute-done.10 = bf16[4,2,16,256]{3,2,1,0:T(8,128)(2,1)S(1)} collective-permute-done((bf16[4,2,16,256]{3,2,1,0:T(8,128)(2,1)S(1)}, bf16[4,2,16,256]{3,2,1,0:T(8,128)(2,1)S(1)}, u32[]{:S(2)}, u32[]{:S(2)}) %collective-permute-start.10) | collective-permute-done | bytes 65568 | tf_op jit(solution)/shard_map/ppermute | solution.py:45
  29.0 1.6 %collective-permute-start.12 = (bf16[2,4,2,16,256]{4,3,2,1,0:T(8,128)(2,1)S(1)}, bf16[2,4,2,16,256]{4,3,2,1,0:T(8,128)(2,1)S(1)}, u32[]{:S(2)}, u32[]{:S(2)}) collective-permute-start(bf16[2,4,2,16,256]{4,3,2,1,0:T(8,128)(2,1)S(1)} %pad_maximum_fusion.1.chip), channel_id=1, source_target_pairs={{0,1},{1,0},{2,6},{3,7},{4,5},{5,4},{6,2},{7,3},{8,9},{9,8},{10,14... | collective-permute-start | bytes 393224 | tf_op jit(solution)/shard_map/ppermute | solution.py:45
  30.6 1.5 %collective-permute-start.11 = (bf16[4,2,16,256]{3,2,1,0:T(8,128)(2,1)S(1)}, bf16[4,2,16,256]{3,2,1,0:T(8,128)(2,1)S(1)}, u32[]{:S(2)}, u32[]{:S(2)}) collective-permute-start(bf16[4,2,16,256]{3,2,1,0:T(8,128)(2,1)S(1)} %get-tuple-element.15), channel_id=1, source_target_pairs={{0,5},{1,4},{2,7},{3,6},{4,1},{5,0},{6,3},{7,2},{8,13},{9,12},{10,... | collective-permute-start | bytes 196616 | tf_op jit(solution)/shard_map/ppermute | solution.py:45
  32.1 4.3 %collective-permute-done.11 = bf16[4,2,16,256]{3,2,1,0:T(8,128)(2,1)S(1)} collective-permute-done((bf16[4,2,16,256]{3,2,1,0:T(8,128)(2,1)S(1)}, bf16[4,2,16,256]{3,2,1,0:T(8,128)(2,1)S(1)}, u32[]{:S(2)}, u32[]{:S(2)}) %collective-permute-start.11) | collective-permute-done | bytes 65568 | tf_op jit(solution)/shard_map/ppermute | solution.py:45
  36.4 0.0 collective-permute-done.12
  36.4 0.1 collective-permute-start.13
  36.5 0.0 copy-done.4
  36.5 0.7 %skip.1 = (f32[2,512,512]{2,1,0:T(8,128)S(1)}, bf16[512,256]{1,0:T(8,128)(2,1)S(1)}) custom-call(bf16[2,512,512]{2,1,0:T(8,128)(2,1)S(1)} %bitcast.25, bf16[512,512]{1,0:T(8,128)(2,1)S(1)} %copy-done.4), custom_call_target="tpu_custom_call" | custom-call | flops 536870912 | bytes 1048576 | tf_op jit(solution)/shard_map/skip/pallas_call | solution.py:257
  37.3 0.7 %collective-permute-done.13.theirs = bf16[3,4,2,16,256]{4,3,2,1,0:T(8,128)(2,1)S(1)} collective-permute-done((bf16[3,4,2,16,256]{4,3,2,1,0:T(8,128)(2,1)S(1)}, bf16[3,4,2,16,256]{4,3,2,1,0:T(8,128)(2,1)S(1)}, u32[]{:S(2)}, u32[]{:S(2)}) %collective-permute-start.13) | collective-permute-done | bytes 196640 | tf_op jit(solution)/shard_map/ppermute | solution.py:45
  38.0 0.0 copy-done.2
  38.0 0.0 copy-done.3
  38.0 4.3 %output.1 = bf16[2,512,512]{2,1,0:T(8,128)(2,1)} custom-call(bf16[2,4,2,16,256]{4,3,2,1,0:T(8,128)(2,1)S(1)} %pad_maximum_fusion.1.chip, bf16[3,4,2,16,256]{4,3,2,1,0:T(8,128)(2,1)S(1)} %pad_maximum_fusion.mine, bf16[3,4,2,16,256]{4,3,2,1,0:T(8,128)(2,1)S(1)} %collective-permute-done.13.theirs, f32[2,512,512]{2,1,0:T(8,128)S(1)} %get-tuple-element.7.skip, ...), custom_call_target="tpu_custom_call" | custom-call | flops 2415919104 | bytes 2097152 | tf_op jit(solution)/shard_map/output/pallas_call | solution.py:329
  (9 shorter events, 0.1 us)
Async XLA Ops:
  0.0 1.2 %copy-start.1 = (bf16[2,16,32,512]{3,2,1,0:T(8,128)(2,1)S(1)}, bf16[2,16,32,512]{3,2,1,0:T(8,128)(2,1)}, u32[]{:S(2)}) copy-start(bf16[2,16,32,512]{3,2,1,0:T(8,128)(2,1)} %param.5) | copy-start | bytes 3145732
  1.5 18.7 %copy-start = (bf16[8,2,512,256]{3,2,1,0:T(8,128)(2,1)S(1)}, bf16[8,2,512,256]{3,2,1,0:T(8,128)(2,1)}, u32[]{:S(2)}) copy-start(bf16[8,2,512,256]{3,2,1,0:T(8,128)(2,1)} %weight.1) | copy-start | bytes 12582916
  1.5 1.7 %collective-permute-start = (bf16[2,128,512]{2,1,0:T(8,128)(2,1)S(1)}, bf16[2,128,512]{2,1,0:T(8,128)(2,1)S(1)}, u32[]{:S(2)}, u32[]{:S(2)}) collective-permute-start(bf16[2,128,512]{2,1,0:T(8,128)(2,1)S(1)} %forward.3), channel_id=1, source_target_pairs={{0,2},{1,3},{2,0},{3,1},{4,6},{5,7},{6,4},{7,5},{8,10},{9,11},{10,... | collective-permute-start | bytes 786440 | tf_op jit(solution)/shard_map/ppermute | solution.py:45
  2.4 34.1 %copy-start.4 = (bf16[512,512]{1,0:T(8,128)(2,1)S(1)}, bf16[512,512]{1,0:T(8,128)(2,1)}, u32[]{:S(2)}) copy-start(bf16[512,512]{1,0:T(8,128)(2,1)} %skip_weight.1) | copy-start | bytes 1572868
  3.3 34.6 %copy-start.2 = (bf16[1024,512]{1,0:T(8,128)(2,1)S(1)}, bf16[1024,512]{1,0:T(8,128)(2,1)}, u32[]{:S(2)}) copy-start(bf16[1024,512]{1,0:T(8,128)(2,1)} %inner_weight.1) | copy-start | bytes 3145732
  3.4 34.6 %copy-start.3 = (bf16[1024,512]{1,0:T(8,128)(2,1)S(1)}, bf16[1024,512]{1,0:T(8,128)(2,1)}, u32[]{:S(2)}) copy-start(bf16[1024,512]{1,0:T(8,128)(2,1)} %outer_weight.1) | copy-start | bytes 3145732
  3.4 7.3 %collective-permute-start.1 = (bf16[2,2,16,512]{3,2,0,1:T(8,128)(2,1)S(1)}, bf16[2,2,16,512]{3,2,0,1:T(8,128)(2,1)S(1)}, u32[]{:S(2)}, u32[]{:S(2)}) collective-permute-start(bf16[2,2,16,512]{3,2,0,1:T(8,128)(2,1)S(1)} %get-tuple-element.11), channel_id=1, source_target_pairs={{0,16},{1,17},{2,30},{3,31},{4,20},{5,21},{6,26},{7,27},{8,24},{9,... | collective-permute-start | bytes 196616 | tf_op jit(solution)/shard_map/ppermute | solution.py:45
  7.4 4.5 %collective-permute-start.3 = (bf16[2,2,16,512]{3,2,0,1:T(8,128)(2,1)S(1)}, bf16[2,2,16,512]{3,2,0,1:T(8,128)(2,1)S(1)}, u32[]{:S(2)}, u32[]{:S(2)}) collective-permute-start(bf16[2,2,16,512]{3,2,0,1:T(8,128)(2,1)S(1)} %get-tuple-element.12), channel_id=1, source_target_pairs={{0,4},{1,5},{2,14},{3,15},{4,0},{5,1},{6,10},{7,11},{8,12},{9,13},... | collective-permute-start | bytes 196616 | tf_op jit(solution)/shard_map/ppermute | solution.py:45
  8.9 5.0 %collective-permute-start.2 = (bf16[2,2,16,512]{3,2,0,1:T(8,128)(2,1)S(1)}, bf16[2,2,16,512]{3,2,0,1:T(8,128)(2,1)S(1)}, u32[]{:S(2)}, u32[]{:S(2)}) collective-permute-start(bf16[2,2,16,512]{3,2,0,1:T(8,128)(2,1)S(1)} %get-tuple-element.13), channel_id=1, source_target_pairs={{0,8},{1,9},{2,22},{3,23},{4,12},{5,13},{6,18},{7,19},{8,0},{9,1},... | collective-permute-start | bytes 196616 | tf_op jit(solution)/shard_map/ppermute | solution.py:45
  10.5 5.7 %collective-permute-start.4 = (bf16[2,16,512]{2,1,0:T(8,128)(2,1)S(1)}, bf16[2,16,512]{2,1,0:T(8,128)(2,1)S(1)}, u32[]{:S(2)}, u32[]{:S(2)}) collective-permute-start(bf16[2,16,512]{2,1,0:T(8,128)(2,1)S(1)} %slice_bitcast_fusion), channel_id=1, source_target_pairs={{0,24},{1,25},{2,26},{3,27},{4,28},{5,29},{6,30},{7,31},{8,16},{9,... | collective-permute-start | bytes 98312 | tf_op jit(solution)/shard_map/ppermute | solution.py:45
  14.0 2.3 %collective-permute-start.5 = (bf16[2,16,512]{2,1,0:T(8,128)(2,1)S(1)}, bf16[2,16,512]{2,1,0:T(8,128)(2,1)S(1)}, u32[]{:S(2)}, u32[]{:S(2)}) collective-permute-start(bf16[2,16,512]{2,1,0:T(8,128)(2,1)S(1)} %fusion.3), channel_id=1, source_target_pairs={{0,2},{1,3},{2,0},{3,1},{4,6},{5,7},{6,4},{7,5},{8,10},{9,11},{10,... | collective-permute-start | bytes 98312 | tf_op jit(solution)/shard_map/ppermute | solution.py:45
  16.3 4.0 %collective-permute-start.6 = (bf16[2,16,512]{2,1,0:T(8,128)(2,1)S(1)}, bf16[2,16,512]{2,1,0:T(8,128)(2,1)S(1)}, u32[]{:S(2)}, u32[]{:S(2)}) collective-permute-start(bf16[2,16,512]{2,1,0:T(8,128)(2,1)S(1)} %get-tuple-element.9), channel_id=1, source_target_pairs={{0,1},{1,0},{2,3},{3,2},{4,5},{5,4},{6,7},{7,6},{8,9},{9,8},{10,11... | collective-permute-start | bytes 98312 | tf_op jit(solution)/shard_map/ppermute | solution.py:45
  21.1 1.2 %collective-permute-start.8 = (bf16[1,2,16,256]{3,2,1,0:T(8,128)(2,1)S(1)}, bf16[1,2,16,256]{3,2,1,0:T(8,128)(2,1)S(1)}, u32[]{:S(2)}, u32[]{:S(2)}) collective-permute-start(bf16[1,2,16,256]{3,2,1,0:T(8,128)(2,1)S(1)} %bitcast.19), channel_id=1, source_target_pairs={{0,2},{1,3},{2,0},{3,1},{4,6},{5,7},{6,4},{7,5},{8,10},{9,11},{10,... | collective-permute-start | bytes 49160 | tf_op jit(solution)/shard_map/ppermute | solution.py:45
  22.3 5.3 %collective-permute-start.9 = (bf16[2,2,16,256]{3,2,1,0:T(8,128)(2,1)S(1)}, bf16[2,2,16,256]{3,2,1,0:T(8,128)(2,1)S(1)}, u32[]{:S(2)}, u32[]{:S(2)}) collective-permute-start(bf16[2,2,16,256]{3,2,1,0:T(8,128)(2,1)S(1)} %pad_maximum_fusion.3), channel_id=1, source_target_pairs={{0,8},{1,9},{2,26},{3,27},{4,12},{5,13},{6,30},{7,31},{8,0},{9,1},... | collective-permute-start | bytes 98312 | tf_op jit(solution)/shard_map/ppermute | solution.py:45
  23.0 4.7 %collective-permute-start.7 = (bf16[1,2,16,256]{3,2,1,0:T(8,128)(2,1)S(1)}, bf16[1,2,16,256]{3,2,1,0:T(8,128)(2,1)S(1)}, u32[]{:S(2)}, u32[]{:S(2)}) collective-permute-start(bf16[1,2,16,256]{3,2,1,0:T(8,128)(2,1)S(1)} %bitcast.21), channel_id=1, source_target_pairs={{0,16},{1,17},{2,18},{3,19},{4,20},{5,21},{6,22},{7,23},{8,24},{9,... | collective-permute-start | bytes 49160 | tf_op jit(solution)/shard_map/ppermute | solution.py:45
  27.7 1.3 %collective-permute-start.10 = (bf16[4,2,16,256]{3,2,1,0:T(8,128)(2,1)S(1)}, bf16[4,2,16,256]{3,2,1,0:T(8,128)(2,1)S(1)}, u32[]{:S(2)}, u32[]{:S(2)}) collective-permute-start(bf16[4,2,16,256]{3,2,1,0:T(8,128)(2,1)S(1)} %get-tuple-element.15), channel_id=1, source_target_pairs={{0,2},{1,3},{2,0},{3,1},{4,6},{5,7},{6,4},{7,5},{8,10},{9,11},{10,... | collective-permute-start | bytes 196616 | tf_op jit(solution)/shard_map/ppermute | solution.py:45
  29.0 7.4 %collective-permute-start.12 = (bf16[2,4,2,16,256]{4,3,2,1,0:T(8,128)(2,1)S(1)}, bf16[2,4,2,16,256]{4,3,2,1,0:T(8,128)(2,1)S(1)}, u32[]{:S(2)}, u32[]{:S(2)}) collective-permute-start(bf16[2,4,2,16,256]{4,3,2,1,0:T(8,128)(2,1)S(1)} %pad_maximum_fusion.1.chip), channel_id=1, source_target_pairs={{0,1},{1,0},{2,6},{3,7},{4,5},{5,4},{6,2},{7,3},{8,9},{9,8},{10,14... | collective-permute-start | bytes 393224 | tf_op jit(solution)/shard_map/ppermute | solution.py:45
  30.6 5.8 %collective-permute-start.11 = (bf16[4,2,16,256]{3,2,1,0:T(8,128)(2,1)S(1)}, bf16[4,2,16,256]{3,2,1,0:T(8,128)(2,1)S(1)}, u32[]{:S(2)}, u32[]{:S(2)}) collective-permute-start(bf16[4,2,16,256]{3,2,1,0:T(8,128)(2,1)S(1)} %get-tuple-element.15), channel_id=1, source_target_pairs={{0,5},{1,4},{2,7},{3,6},{4,1},{5,0},{6,3},{7,2},{8,13},{9,12},{10,... | collective-permute-start | bytes 196616 | tf_op jit(solution)/shard_map/ppermute | solution.py:45
  36.4 1.5 %collective-permute-start.13 = (bf16[3,4,2,16,256]{4,3,2,1,0:T(8,128)(2,1)S(1)}, bf16[3,4,2,16,256]{4,3,2,1,0:T(8,128)(2,1)S(1)}, u32[]{:S(2)}, u32[]{:S(2)}) collective-permute-start(bf16[3,4,2,16,256]{4,3,2,1,0:T(8,128)(2,1)S(1)} %pad_maximum_fusion.mine), channel_id=1, source_target_pairs={{0,2},{1,3},{2,0},{3,1},{4,6},{5,7},{6,4},{7,5},{8,10},{9,11},{10,... | collective-permute-start | bytes 589832 | tf_op jit(solution)/shard_map/ppermute | solution.py:45

commit v3 on v2

--- a/solution.py
+++ b/solution.py
@@ -313,8 +313,10 @@
     planes = []
     for one, two in pairs:
         planes.append(exchange(chip, (2 * one[0], 2 * two[0]), (one[1], two[1])))
-    mine = jnp.concatenate([shared_plane[None]] + planes)
-    theirs = exchange(mine, (1, 1))
+    shared_theirs = exchange(shared_plane, (1, 1))
+    mine = jnp.concatenate(planes)
+    theirs = jnp.concatenate([shared_theirs[None], exchange(mine, (1, 1))])
+    mine = jnp.concatenate([shared_plane[None], mine])
 
     rows = 2 * own_count
     parts = y_devices

time: 42.4 us -> 42.2 us (level)
    ppermute x14 -> x15, waiting for transfers between devices: 18.2 us -> 18 us  [exchange(): return lax.ppermute(value, ('gx', 'gy'), pairs)]
    ppermute x14 -> x15, starting transfers between devices: 16 us -> 15.9 us  [exchange(): return lax.ppermute(value, ('gx', 'gy'), pairs)]
  transfers between devices with their start and end apart: 14 -> 15, of which waited for: 10 -> 11; matrix products, arithmetic and copies ran while one was open for 0% -> 0% of each run, Pallas kernels for 2% -> 2%
where the time goes in v3:
time: 42.2 us; the launch traced here: 42 us
  waiting for transfers between devices  18 us (43%)
  starting transfers between devices  15.9 us (38%)
  Pallas kernels  6.71 us (16%)
  local copies, waits for them, and re-layouts  1.02 us (2%)
    ppermute x15, waiting for transfers between devices, exchange(): return lax.ppermute(value, ('gx', 'gy'), pairs)  18 us
    ppermute x15, starting transfers between devices, exchange(): return lax.ppermute(value, ('gx', 'gy'), pairs)  15.9 us
    pallas_call x1, Pallas kernels, local(): pl.pallas_call(functools.partial(output_kernel, 1.0 / math.sqrt(mode_coun...  4.29 us
    unnamed x10, local copies, waits for them, and re-layouts  0.98 us
  transfers between devices with their start and end apart: 15, of which 11 were waited for; matrix products, arithmetic and copies ran while one was open for 0% of the time, Pallas kernels for 2%

profile of v3, /device:TPU:0, one launch (start us, length us, event | category | flops | bytes accessed | tf_op | source)
XLA Modules:
  0.0 42.0 jit_solution(14509103973140522174)
XLA Ops:
  0.0 0.0 copy-start.1
  0.0 0.3 basis.1
  0.3 1.0 %copy-done.1 = bf16[2,16,32,512]{3,2,1,0:T(8,128)(2,1)S(1)} copy-done((bf16[2,16,32,512]{3,2,1,0:T(8,128)(2,1)S(1)}, bf16[2,16,32,512]{3,2,1,0:T(8,128)(2,1)}, u32[]{:S(2)}) %copy-start.1) | copy-done | bytes 1048600
  1.2 0.3 forward.3
  1.5 0.0 copy-start
  1.5 0.6 %collective-permute-start = (bf16[2,128,512]{2,1,0:T(8,128)(2,1)S(1)}, bf16[2,128,512]{2,1,0:T(8,128)(2,1)S(1)}, u32[]{:S(2)}, u32[]{:S(2)}) collective-permute-start(bf16[2,128,512]{2,1,0:T(8,128)(2,1)S(1)} %forward.3), channel_id=1, source_target_pairs={{0,2},{1,3},{2,0},{3,1},{4,6},{5,7},{6,4},{7,5},{8,10},{9,11},{10,... | collective-permute-start | bytes 786440 | tf_op jit(solution)/shard_map/ppermute | solution.py:45
  2.1 0.3 forward.2
  2.4 0.0 copy-start.4
  2.4 0.8 %collective-permute-done = bf16[2,128,512]{2,1,0:T(8,128)(2,1)S(1)} collective-permute-done((bf16[2,128,512]{2,1,0:T(8,128)(2,1)S(1)}, bf16[2,128,512]{2,1,0:T(8,128)(2,1)S(1)}, u32[]{:S(2)}, u32[]{:S(2)}) %collective-permute-start) | collective-permute-done | bytes 262176 | tf_op jit(solution)/shard_map/ppermute | solution.py:45
  3.3 0.1 convert_add_fusion
  3.4 0.0 copy-start.2
  3.4 0.0 copy-start.3
  3.4 4.0 %collective-permute-start.1 = (bf16[2,2,16,512]{3,2,0,1:T(8,128)(2,1)S(1)}, bf16[2,2,16,512]{3,2,0,1:T(8,128)(2,1)S(1)}, u32[]{:S(2)}, u32[]{:S(2)}) collective-permute-start(bf16[2,2,16,512]{3,2,0,1:T(8,128)(2,1)S(1)} %get-tuple-element.11), channel_id=1, source_target_pairs={{0,16},{1,17},{2,30},{3,31},{4,20},{5,21},{6,26},{7,27},{8,24},{9,... | collective-permute-start | bytes 196616 | tf_op jit(solution)/shard_map/ppermute | solution.py:45
  7.4 1.5 %collective-permute-start.3 = (bf16[2,2,16,512]{3,2,0,1:T(8,128)(2,1)S(1)}, bf16[2,2,16,512]{3,2,0,1:T(8,128)(2,1)S(1)}, u32[]{:S(2)}, u32[]{:S(2)}) collective-permute-start(bf16[2,2,16,512]{3,2,0,1:T(8,128)(2,1)S(1)} %get-tuple-element.12), channel_id=1, source_target_pairs={{0,4},{1,5},{2,14},{3,15},{4,0},{5,1},{6,10},{7,11},{8,12},{9,13},... | collective-permute-start | bytes 196616 | tf_op jit(solution)/shard_map/ppermute | solution.py:45
  8.9 1.6 %collective-permute-start.2 = (bf16[2,2,16,512]{3,2,0,1:T(8,128)(2,1)S(1)}, bf16[2,2,16,512]{3,2,0,1:T(8,128)(2,1)S(1)}, u32[]{:S(2)}, u32[]{:S(2)}) collective-permute-start(bf16[2,2,16,512]{3,2,0,1:T(8,128)(2,1)S(1)} %get-tuple-element.13), channel_id=1, source_target_pairs={{0,8},{1,9},{2,22},{3,23},{4,12},{5,13},{6,18},{7,19},{8,0},{9,1},... | collective-permute-start | bytes 196616 | tf_op jit(solution)/shard_map/ppermute | solution.py:45
  10.5 0.2 collective-permute-start.4
  10.7 0.0 collective-permute-done.1
  10.8 1.1 %collective-permute-done.3 = bf16[2,2,16,512]{3,2,0,1:T(8,128)(2,1)S(1)} collective-permute-done((bf16[2,2,16,512]{3,2,0,1:T(8,128)(2,1)S(1)}, bf16[2,2,16,512]{3,2,0,1:T(8,128)(2,1)S(1)}, u32[]{:S(2)}, u32[]{:S(2)}) %collective-permute-start.3) | collective-permute-done | bytes 65568 | tf_op jit(solution)/shard_map/ppermute | solution.py:45
  11.9 2.0 %collective-permute-done.2 = bf16[2,2,16,512]{3,2,0,1:T(8,128)(2,1)S(1)} collective-permute-done((bf16[2,2,16,512]{3,2,0,1:T(8,128)(2,1)S(1)}, bf16[2,2,16,512]{3,2,0,1:T(8,128)(2,1)S(1)}, u32[]{:S(2)}, u32[]{:S(2)}) %collective-permute-start.2) | collective-permute-done | bytes 65568 | tf_op jit(solution)/shard_map/ppermute | solution.py:45
  14.0 0.7 %collective-permute-start.5 = (bf16[2,16,512]{2,1,0:T(8,128)(2,1)S(1)}, bf16[2,16,512]{2,1,0:T(8,128)(2,1)S(1)}, u32[]{:S(2)}, u32[]{:S(2)}) collective-permute-start(bf16[2,16,512]{2,1,0:T(8,128)(2,1)S(1)} %fusion.3), channel_id=1, source_target_pairs={{0,2},{1,3},{2,0},{3,1},{4,6},{5,7},{6,4},{7,5},{8,10},{9,11},{10,... | collective-permute-start | bytes 98312 | tf_op jit(solution)/shard_map/ppermute | solution.py:45
  14.6 1.6 %collective-permute-done.4 = bf16[2,16,512]{2,1,0:T(8,128)(2,1)S(1)} collective-permute-done((bf16[2,16,512]{2,1,0:T(8,128)(2,1)S(1)}, bf16[2,16,512]{2,1,0:T(8,128)(2,1)S(1)}, u32[]{:S(2)}, u32[]{:S(2)}) %collective-permute-start.4) | collective-permute-done | bytes 32800 | tf_op jit(solution)/shard_map/ppermute | solution.py:45
  16.2 0.0 collective-permute-done.5
  16.3 1.6 %collective-permute-start.6 = (bf16[2,16,512]{2,1,0:T(8,128)(2,1)S(1)}, bf16[2,16,512]{2,1,0:T(8,128)(2,1)S(1)}, u32[]{:S(2)}, u32[]{:S(2)}) collective-permute-start(bf16[2,16,512]{2,1,0:T(8,128)(2,1)S(1)} %get-tuple-element.9), channel_id=1, source_target_pairs={{0,1},{1,0},{2,3},{3,2},{4,5},{5,4},{6,7},{7,6},{8,9},{9,8},{10,11... | collective-permute-start | bytes 98312 | tf_op jit(solution)/shard_map/ppermute | solution.py:45
  17.8 2.4 %collective-permute-done.6.other = bf16[2,16,512]{2,1,0:T(8,128)(2,1)S(1)} collective-permute-done((bf16[2,16,512]{2,1,0:T(8,128)(2,1)S(1)}, bf16[2,16,512]{2,1,0:T(8,128)(2,1)S(1)}, u32[]{:S(2)}, u32[]{:S(2)}) %collective-permute-start.6) | collective-permute-done | bytes 32800 | tf_op jit(solution)/shard_map/ppermute | solution.py:45
  20.2 0.0 copy-done
  20.2 0.8 %mix.1 = bf16[2,16,256]{2,1,0:T(8,128)(2,1)S(1)} custom-call(f32[2,16,512]{2,1,0:T(8,128)S(1)} %get-tuple-element.10.total, bf16[2,16,512]{2,1,0:T(8,128)(2,1)S(1)} %collective-permute-done.6.other, bf16[8,2,512,256]{3,2,1,0:T(8,128)(2,1)S(1)} %copy-done), custom_call_target="tpu_custom_call" | custom-call | flops 16777216 | bytes 4194304 | tf_op jit(solution)/shard_map/mix/pallas_call | solution.py:290
  21.1 0.1 collective-permute-start.8
  21.1 1.2 %collective-permute-done.8 = bf16[1,2,16,256]{3,2,1,0:T(8,128)(2,1)S(1)} collective-permute-done((bf16[1,2,16,256]{3,2,1,0:T(8,128)(2,1)S(1)}, bf16[1,2,16,256]{3,2,1,0:T(8,128)(2,1)S(1)}, u32[]{:S(2)}, u32[]{:S(2)}) %collective-permute-start.8) | collective-permute-done | bytes 16416 | tf_op jit(solution)/shard_map/ppermute | solution.py:45
  22.3 0.7 %collective-permute-start.9 = (bf16[2,2,16,256]{3,2,1,0:T(8,128)(2,1)S(1)}, bf16[2,2,16,256]{3,2,1,0:T(8,128)(2,1)S(1)}, u32[]{:S(2)}, u32[]{:S(2)}) collective-permute-start(bf16[2,2,16,256]{3,2,1,0:T(8,128)(2,1)S(1)} %pad_maximum_fusion.4), channel_id=1, source_target_pairs={{0,8},{1,9},{2,26},{3,27},{4,12},{5,13},{6,30},{7,31},{8,0},{9,1},... | collective-permute-start | bytes 98312 | tf_op jit(solution)/shard_map/ppermute | solution.py:45
  23.0 1.8 %collective-permute-start.7 = (bf16[1,2,16,256]{3,2,1,0:T(8,128)(2,1)S(1)}, bf16[1,2,16,256]{3,2,1,0:T(8,128)(2,1)S(1)}, u32[]{:S(2)}, u32[]{:S(2)}) collective-permute-start(bf16[1,2,16,256]{3,2,1,0:T(8,128)(2,1)S(1)} %bitcast.22), channel_id=1, source_target_pairs={{0,16},{1,17},{2,18},{3,19},{4,20},{5,21},{6,22},{7,23},{8,24},{9,... | collective-permute-start | bytes 49160 | tf_op jit(solution)/shard_map/ppermute | solution.py:45
  24.8 2.8 %collective-permute-done.7 = bf16[1,2,16,256]{3,2,1,0:T(8,128)(2,1)S(1)} collective-permute-done((bf16[1,2,16,256]{3,2,1,0:T(8,128)(2,1)S(1)}, bf16[1,2,16,256]{3,2,1,0:T(8,128)(2,1)S(1)}, u32[]{:S(2)}, u32[]{:S(2)}) %collective-permute-start.7) | collective-permute-done | bytes 16416 | tf_op jit(solution)/shard_map/ppermute | solution.py:45
  27.7 0.0 collective-permute-done.9
  27.7 0.2 collective-permute-start.10
  27.9 1.1 %collective-permute-done.10 = bf16[4,2,16,256]{3,2,1,0:T(8,128)(2,1)S(1)} collective-permute-done((bf16[4,2,16,256]{3,2,1,0:T(8,128)(2,1)S(1)}, bf16[4,2,16,256]{3,2,1,0:T(8,128)(2,1)S(1)}, u32[]{:S(2)}, u32[]{:S(2)}) %collective-permute-start.10) | collective-permute-done | bytes 65568 | tf_op jit(solution)/shard_map/ppermute | solution.py:45
  29.0 1.6 %collective-permute-start.12 = (bf16[2,4,2,16,256]{4,3,2,1,0:T(8,128)(2,1)S(1)}, bf16[2,4,2,16,256]{4,3,2,1,0:T(8,128)(2,1)S(1)}, u32[]{:S(2)}, u32[]{:S(2)}) collective-permute-start(bf16[2,4,2,16,256]{4,3,2,1,0:T(8,128)(2,1)S(1)} %pad_maximum_fusion.2.chip), channel_id=1, source_target_pairs={{0,1},{1,0},{2,6},{3,7},{4,5},{5,4},{6,2},{7,3},{8,9},{9,8},{10,14... | collective-permute-start | bytes 393224 | tf_op jit(solution)/shard_map/ppermute | solution.py:45
  30.6 1.5 %collective-permute-start.11 = (bf16[4,2,16,256]{3,2,1,0:T(8,128)(2,1)S(1)}, bf16[4,2,16,256]{3,2,1,0:T(8,128)(2,1)S(1)}, u32[]{:S(2)}, u32[]{:S(2)}) collective-permute-start(bf16[4,2,16,256]{3,2,1,0:T(8,128)(2,1)S(1)} %get-tuple-element.15), channel_id=1, source_target_pairs={{0,5},{1,4},{2,7},{3,6},{4,1},{5,0},{6,3},{7,2},{8,13},{9,12},{10,... | collective-permute-start | bytes 196616 | tf_op jit(solution)/shard_map/ppermute | solution.py:45
  32.1 2.7 %collective-permute-done.12 = bf16[2,4,2,16,256]{4,3,2,1,0:T(8,128)(2,1)S(1)} collective-permute-done((bf16[2,4,2,16,256]{4,3,2,1,0:T(8,128)(2,1)S(1)}, bf16[2,4,2,16,256]{4,3,2,1,0:T(8,128)(2,1)S(1)}, u32[]{:S(2)}, u32[]{:S(2)}) %collective-permute-start.12) | collective-permute-done | bytes 131104 | tf_op jit(solution)/shard_map/ppermute | solution.py:45
  34.7 0.0 collective-permute-start.14
  34.7 0.0 copy-done.4
  34.8 0.7 %skip.1 = (f32[2,512,512]{2,1,0:T(8,128)S(1)}, bf16[512,256]{1,0:T(8,128)(2,1)S(1)}) custom-call(bf16[2,512,512]{2,1,0:T(8,128)(2,1)S(1)} %bitcast.26, bf16[512,512]{1,0:T(8,128)(2,1)S(1)} %copy-done.4), custom_call_target="tpu_custom_call" | custom-call | flops 536870912 | bytes 1048576 | tf_op jit(solution)/shard_map/skip/pallas_call | solution.py:257
  35.5 0.9 %collective-permute-done.11 = bf16[4,2,16,256]{3,2,1,0:T(8,128)(2,1)S(1)} collective-permute-done((bf16[4,2,16,256]{3,2,1,0:T(8,128)(2,1)S(1)}, bf16[4,2,16,256]{3,2,1,0:T(8,128)(2,1)S(1)}, u32[]{:S(2)}, u32[]{:S(2)}) %collective-permute-start.11) | collective-permute-done | bytes 65568 | tf_op jit(solution)/shard_map/ppermute | solution.py:45
  36.4 0.0 collective-permute-start.13
  36.4 1.2 %collective-permute-done.13 = bf16[4,2,16,256]{3,2,1,0:T(8,128)(2,1)S(1)} collective-permute-done((bf16[4,2,16,256]{3,2,1,0:T(8,128)(2,1)S(1)}, bf16[4,2,16,256]{3,2,1,0:T(8,128)(2,1)S(1)}, u32[]{:S(2)}, u32[]{:S(2)}) %collective-permute-start.13) | collective-permute-done | bytes 65568 | tf_op jit(solution)/shard_map/ppermute | solution.py:45
  37.7 0.0 collective-permute-done.14
  37.7 0.0 copy-done.2
  37.7 0.0 copy-done.3
  37.7 4.3 %output.1 = bf16[2,512,512]{2,1,0:T(8,128)(2,1)} custom-call(bf16[2,4,2,16,256]{4,3,2,1,0:T(8,128)(2,1)S(1)} %pad_maximum_fusion.2.chip, bf16[3,4,2,16,256]{4,3,2,1,0:T(8,128)(2,1)S(1)} %pad_maximum_fusion.mine, bf16[3,4,2,16,256]{4,3,2,1,0:T(8,128)(2,1)S(1)} %pad_maximum_fusion.1.theirs, f32[2,512,512]{2,1,0:T(8,128)S(1)} %get-tuple-element.7.skip, ...), custom_call_target="tpu_custom_call" | custom-call | flops 2415919104 | bytes 2097152 | tf_op jit(solution)/shard_map/output/pallas_call | solution.py:331
  (10 shorter events, 0.2 us)
Async XLA Ops:
  0.0 1.2 %copy-start.1 = (bf16[2,16,32,512]{3,2,1,0:T(8,128)(2,1)S(1)}, bf16[2,16,32,512]{3,2,1,0:T(8,128)(2,1)}, u32[]{:S(2)}) copy-start(bf16[2,16,32,512]{3,2,1,0:T(8,128)(2,1)} %param.5) | copy-start | bytes 3145732
  1.5 18.7 %copy-start = (bf16[8,2,512,256]{3,2,1,0:T(8,128)(2,1)S(1)}, bf16[8,2,512,256]{3,2,1,0:T(8,128)(2,1)}, u32[]{:S(2)}) copy-start(bf16[8,2,512,256]{3,2,1,0:T(8,128)(2,1)} %weight.1) | copy-start | bytes 12582916
  1.5 1.7 %collective-permute-start = (bf16[2,128,512]{2,1,0:T(8,128)(2,1)S(1)}, bf16[2,128,512]{2,1,0:T(8,128)(2,1)S(1)}, u32[]{:S(2)}, u32[]{:S(2)}) collective-permute-start(bf16[2,128,512]{2,1,0:T(8,128)(2,1)S(1)} %forward.3), channel_id=1, source_target_pairs={{0,2},{1,3},{2,0},{3,1},{4,6},{5,7},{6,4},{7,5},{8,10},{9,11},{10,... | collective-permute-start | bytes 786440 | tf_op jit(solution)/shard_map/ppermute | solution.py:45
  2.4 32.3 %copy-start.4 = (bf16[512,512]{1,0:T(8,128)(2,1)S(1)}, bf16[512,512]{1,0:T(8,128)(2,1)}, u32[]{:S(2)}) copy-start(bf16[512,512]{1,0:T(8,128)(2,1)} %skip_weight.1) | copy-start | bytes 1572868
  3.4 34.3 %copy-start.2 = (bf16[1024,512]{1,0:T(8,128)(2,1)S(1)}, bf16[1024,512]{1,0:T(8,128)(2,1)}, u32[]{:S(2)}) copy-start(bf16[1024,512]{1,0:T(8,128)(2,1)} %inner_weight.1) | copy-start | bytes 3145732
  3.4 34.3 %copy-start.3 = (bf16[1024,512]{1,0:T(8,128)(2,1)S(1)}, bf16[1024,512]{1,0:T(8,128)(2,1)}, u32[]{:S(2)}) copy-start(bf16[1024,512]{1,0:T(8,128)(2,1)} %outer_weight.1) | copy-start | bytes 3145732
  3.4 7.3 %collective-permute-start.1 = (bf16[2,2,16,512]{3,2,0,1:T(8,128)(2,1)S(1)}, bf16[2,2,16,512]{3,2,0,1:T(8,128)(2,1)S(1)}, u32[]{:S(2)}, u32[]{:S(2)}) collective-permute-start(bf16[2,2,16,512]{3,2,0,1:T(8,128)(2,1)S(1)} %get-tuple-element.11), channel_id=1, source_target_pairs={{0,16},{1,17},{2,30},{3,31},{4,20},{5,21},{6,26},{7,27},{8,24},{9,... | collective-permute-start | bytes 196616 | tf_op jit(solution)/shard_map/ppermute | solution.py:45
  7.4 4.5 %collective-permute-start.3 = (bf16[2,2,16,512]{3,2,0,1:T(8,128)(2,1)S(1)}, bf16[2,2,16,512]{3,2,0,1:T(8,128)(2,1)S(1)}, u32[]{:S(2)}, u32[]{:S(2)}) collective-permute-start(bf16[2,2,16,512]{3,2,0,1:T(8,128)(2,1)S(1)} %get-tuple-element.12), channel_id=1, source_target_pairs={{0,4},{1,5},{2,14},{3,15},{4,0},{5,1},{6,10},{7,11},{8,12},{9,13},... | collective-permute-start | bytes 196616 | tf_op jit(solution)/shard_map/ppermute | solution.py:45
  8.9 5.0 %collective-permute-start.2 = (bf16[2,2,16,512]{3,2,0,1:T(8,128)(2,1)S(1)}, bf16[2,2,16,512]{3,2,0,1:T(8,128)(2,1)S(1)}, u32[]{:S(2)}, u32[]{:S(2)}) collective-permute-start(bf16[2,2,16,512]{3,2,0,1:T(8,128)(2,1)S(1)} %get-tuple-element.13), channel_id=1, source_target_pairs={{0,8},{1,9},{2,22},{3,23},{4,12},{5,13},{6,18},{7,19},{8,0},{9,1},... | collective-permute-start | bytes 196616 | tf_op jit(solution)/shard_map/ppermute | solution.py:45
  10.5 5.7 %collective-permute-start.4 = (bf16[2,16,512]{2,1,0:T(8,128)(2,1)S(1)}, bf16[2,16,512]{2,1,0:T(8,128)(2,1)S(1)}, u32[]{:S(2)}, u32[]{:S(2)}) collective-permute-start(bf16[2,16,512]{2,1,0:T(8,128)(2,1)S(1)} %slice_bitcast_fusion), channel_id=1, source_target_pairs={{0,24},{1,25},{2,26},{3,27},{4,28},{5,29},{6,30},{7,31},{8,16},{9,... | collective-permute-start | bytes 98312 | tf_op jit(solution)/shard_map/ppermute | solution.py:45
  14.0 2.3 %collective-permute-start.5 = (bf16[2,16,512]{2,1,0:T(8,128)(2,1)S(1)}, bf16[2,16,512]{2,1,0:T(8,128)(2,1)S(1)}, u32[]{:S(2)}, u32[]{:S(2)}) collective-permute-start(bf16[2,16,512]{2,1,0:T(8,128)(2,1)S(1)} %fusion.3), channel_id=1, source_target_pairs={{0,2},{1,3},{2,0},{3,1},{4,6},{5,7},{6,4},{7,5},{8,10},{9,11},{10,... | collective-permute-start | bytes 98312 | tf_op jit(solution)/shard_map/ppermute | solution.py:45
  16.3 4.0 %collective-permute-start.6 = (bf16[2,16,512]{2,1,0:T(8,128)(2,1)S(1)}, bf16[2,16,512]{2,1,0:T(8,128)(2,1)S(1)}, u32[]{:S(2)}, u32[]{:S(2)}) collective-permute-start(bf16[2,16,512]{2,1,0:T(8,128)(2,1)S(1)} %get-tuple-element.9), channel_id=1, source_target_pairs={{0,1},{1,0},{2,3},{3,2},{4,5},{5,4},{6,7},{7,6},{8,9},{9,8},{10,11... | collective-permute-start | bytes 98312 | tf_op jit(solution)/shard_map/ppermute | solution.py:45
  21.1 1.2 %collective-permute-start.8 = (bf16[1,2,16,256]{3,2,1,0:T(8,128)(2,1)S(1)}, bf16[1,2,16,256]{3,2,1,0:T(8,128)(2,1)S(1)}, u32[]{:S(2)}, u32[]{:S(2)}) collective-permute-start(bf16[1,2,16,256]{3,2,1,0:T(8,128)(2,1)S(1)} %bitcast.20), channel_id=1, source_target_pairs={{0,2},{1,3},{2,0},{3,1},{4,6},{5,7},{6,4},{7,5},{8,10},{9,11},{10,... | collective-permute-start | bytes 49160 | tf_op jit(solution)/shard_map/ppermute | solution.py:45
  22.3 5.3 %collective-permute-start.9 = (bf16[2,2,16,256]{3,2,1,0:T(8,128)(2,1)S(1)}, bf16[2,2,16,256]{3,2,1,0:T(8,128)(2,1)S(1)}, u32[]{:S(2)}, u32[]{:S(2)}) collective-permute-start(bf16[2,2,16,256]{3,2,1,0:T(8,128)(2,1)S(1)} %pad_maximum_fusion.4), channel_id=1, source_target_pairs={{0,8},{1,9},{2,26},{3,27},{4,12},{5,13},{6,30},{7,31},{8,0},{9,1},... | collective-permute-start | bytes 98312 | tf_op jit(solution)/shard_map/ppermute | solution.py:45
  23.0 4.7 %collective-permute-start.7 = (bf16[1,2,16,256]{3,2,1,0:T(8,128)(2,1)S(1)}, bf16[1,2,16,256]{3,2,1,0:T(8,128)(2,1)S(1)}, u32[]{:S(2)}, u32[]{:S(2)}) collective-permute-start(bf16[1,2,16,256]{3,2,1,0:T(8,128)(2,1)S(1)} %bitcast.22), channel_id=1, source_target_pairs={{0,16},{1,17},{2,18},{3,19},{4,20},{5,21},{6,22},{7,23},{8,24},{9,... | collective-permute-start | bytes 49160 | tf_op jit(solution)/shard_map/ppermute | solution.py:45
  27.7 1.3 %collective-permute-start.10 = (bf16[4,2,16,256]{3,2,1,0:T(8,128)(2,1)S(1)}, bf16[4,2,16,256]{3,2,1,0:T(8,128)(2,1)S(1)}, u32[]{:S(2)}, u32[]{:S(2)}) collective-permute-start(bf16[4,2,16,256]{3,2,1,0:T(8,128)(2,1)S(1)} %get-tuple-element.15), channel_id=1, source_target_pairs={{0,2},{1,3},{2,0},{3,1},{4,6},{5,7},{6,4},{7,5},{8,10},{9,11},{10,... | collective-permute-start | bytes 196616 | tf_op jit(solution)/shard_map/ppermute | solution.py:45
  29.0 5.7 %collective-permute-start.12 = (bf16[2,4,2,16,256]{4,3,2,1,0:T(8,128)(2,1)S(1)}, bf16[2,4,2,16,256]{4,3,2,1,0:T(8,128)(2,1)S(1)}, u32[]{:S(2)}, u32[]{:S(2)}) collective-permute-start(bf16[2,4,2,16,256]{4,3,2,1,0:T(8,128)(2,1)S(1)} %pad_maximum_fusion.2.chip), channel_id=1, source_target_pairs={{0,1},{1,0},{2,6},{3,7},{4,5},{5,4},{6,2},{7,3},{8,9},{9,8},{10,14... | collective-permute-start | bytes 393224 | tf_op jit(solution)/shard_map/ppermute | solution.py:45
  30.6 5.8 %collective-permute-start.11 = (bf16[4,2,16,256]{3,2,1,0:T(8,128)(2,1)S(1)}, bf16[4,2,16,256]{3,2,1,0:T(8,128)(2,1)S(1)}, u32[]{:S(2)}, u32[]{:S(2)}) collective-permute-start(bf16[4,2,16,256]{3,2,1,0:T(8,128)(2,1)S(1)} %get-tuple-element.15), channel_id=1, source_target_pairs={{0,5},{1,4},{2,7},{3,6},{4,1},{5,0},{6,3},{7,2},{8,13},{9,12},{10,... | collective-permute-start | bytes 196616 | tf_op jit(solution)/shard_map/ppermute | solution.py:45
  34.7 2.9 %collective-permute-start.14 = (bf16[2,4,2,16,256]{4,3,2,1,0:T(8,128)(2,1)S(1)}, bf16[2,4,2,16,256]{4,3,2,1,0:T(8,128)(2,1)S(1)}, u32[]{:S(2)}, u32[]{:S(2)}) collective-permute-start(bf16[2,4,2,16,256]{4,3,2,1,0:T(8,128)(2,1)S(1)} %collective-permute-done.12), channel_id=1, source_target_pairs={{0,2},{1,3},{2,0},{3,1},{4,6},{5,7},{6,4},{7,5},{8,10},{9,11},{10,... | collective-permute-start | bytes 393224 | tf_op jit(solution)/shard_map/ppermute | solution.py:45
  36.4 1.3 %collective-permute-start.13 = (bf16[4,2,16,256]{3,2,1,0:T(8,128)(2,1)S(1)}, bf16[4,2,16,256]{3,2,1,0:T(8,128)(2,1)S(1)}, u32[]{:S(2)}, u32[]{:S(2)}) collective-permute-start(bf16[4,2,16,256]{3,2,1,0:T(8,128)(2,1)S(1)} %collective-permute-done.11), channel_id=1, source_target_pairs={{0,2},{1,3},{2,0},{3,1},{4,6},{5,7},{6,4},{7,5},{8,10},{9,11},{10,... | collective-permute-start | bytes 196616 | tf_op jit(solution)/shard_map/ppermute | solution.py:45
